TPU v7x, 256 devices: a whole 4x4x8 slice. The times are simulated.
256 devices in a mesh: grp: 32 (over x, z), sub: 8 (over y, core).
Axes of the slice: x: 4, y: 4, z: 8, core: 2. Of those that a mesh axis runs over, the one named last changes fastest.
Arguments:
- ham_columns: bfloat16 [768, 5, 128, 128], P(('grp', 'sub')), may hold values from -2.2 to 2.2, as said below
- bond_mask: int32 [768, 4], P(('grp', 'sub')), may hold values 0 or 1
- owned_counts: int32 [32, 8], replicated, may hold values from 1 to 3, as said below
- fermi_level: float32 [1], replicated, may hold values from -0.5 to 0.5
Outputs:
- density: bfloat16 [768, 9, 128, 128], P(('grp', 'sub'))
Inputs may be any that keep to these rules, and one draw needn't show every extreme that they name: `ham_columns`: block 0 of every stored block column is symmetric. `bond_mask`: bond lists of slots that hold no cluster are never read. `owned_counts`: along sub, the devices 2k and 2k + 1 of a group own 2 * 2 block columns together, so group g owns clusters g * 16 to (g + 1) * 16 - 1, handed to its devices in order along sub in consecutive runs; no device owns exactly 2; every row has a device that owns 3.
All inputs are finite; a program needn't handle non-finite values. No bound on the sum of `bond_mask` on one device may be relied on, other than what follows from the above.
Results may differ from a plain program's by a relative error of at most 0.0025.
Values may be sent and summed in bfloat16 or wider, within the bound.
No kernel may reach another device: no remote copies, remote signals or barrier semaphores. Data moves between devices by JAX's collectives and lax.ppermute only.
A program may use at most 64 MiB of HBM per device.

v0:
```python
import jax
import jax.numpy as jnp
from jax import lax
from jax.sharding import PartitionSpec as P

COLS_MEAN = 2


spectral_span = 4.0


def extended(array, sides, width):
    for axis, dim in sides:
        size, length = (lax.axis_size(axis), array.shape[dim])
        up = [(i, (i + 1) % size) for i in range(size)]
        down = [(j, i) for i, j in up]
        last = lax.slice_in_dim(array, length - width, length, axis=dim)
        leading = lax.slice_in_dim(array, 0, width, axis=dim)
        before = lax.ppermute(last, axis, up)
        after = lax.ppermute(leading, axis, down)
        array = jnp.concatenate([before, array, after], axis=dim)
    return array


def partner(value, axis, distance):
    mask = 2**distance
    pairs = [(source, source ^ mask) for source in range(lax.axis_size(axis))]
    return lax.ppermute(value, axis, pairs)


def build_tile(window_cols, window_bonds, chemical):
    reach_len = window_bonds.shape[1]
    window_len = window_cols.shape[0]
    block_width = window_cols.shape[2]
    identity = jnp.eye(block_width, dtype=jnp.float32)
    bond_values = window_bonds.astype(jnp.float32)
    living = []
    for member in range(window_len):
        if member == reach_len:
            living.append(jnp.ones((), jnp.float32))
        elif member > reach_len:
            living.append(bond_values[reach_len, member - reach_len - 1])
        else:
            living.append(bond_values[member, reach_len - member - 1])
    rows_list = []
    for row_blk in range(window_len):
        pieces = []
        for col_blk in range(window_len):
            distance = row_blk - col_blk
            weight = living[row_blk] * living[col_blk]
            if distance == 0:
                block_value = (
                    window_cols[row_blk, 0].astype(jnp.float32) - chemical * identity
                ) * weight
            elif 0 < distance <= reach_len:
                block_value = window_cols[col_blk, distance].astype(jnp.float32) * (
                    weight * bond_values[col_blk, distance - 1]
                )
            elif 0 < -distance <= reach_len:
                block_value = window_cols[row_blk, -distance].astype(jnp.float32).T * (
                    weight * bond_values[row_blk, -distance - 1]
                )
            else:
                block_value = jnp.zeros((block_width, block_width), jnp.float32)
            pieces.append(block_value)
        rows_list.append(jnp.concatenate(pieces, axis=1))
    return (jnp.concatenate(rows_list, axis=0) / spectral_span).astype(jnp.bfloat16)


def product(matrix, vector):
    return jnp.dot(matrix, vector.astype(jnp.bfloat16), preferred_element_type=jnp.float32)


def apply_rest(matrix, first_term):
    second = product(matrix, first_term)
    third_term = product(matrix, second)
    return 1.5 * first_term - 0.5 * third_term


def density_column(matrix, window_len, block_width):
    center = (window_len - 1) // 2
    first_term = matrix[:, center * block_width : (center + 1) * block_width].astype(jnp.float32)
    step_one = apply_rest(matrix, first_term)
    step_two = apply_rest(matrix, product(matrix, step_one))
    step_three = apply_rest(matrix, product(matrix, step_two))
    sign_column = 1.5 * step_one - 0.5 * step_three
    above = jnp.zeros((center * block_width, block_width), jnp.float32)
    selector = jnp.concatenate([above, jnp.eye(block_width, dtype=jnp.float32), above], axis=0)
    result = (0.5 * (selector - sign_column)).astype(jnp.bfloat16)
    return result.reshape(window_len, block_width, block_width)


def window_result(run_cols, run_bonds, first_row, chemical):
    window_len = 2 * run_bonds.shape[1] + 1
    block_width = run_cols.shape[2]
    window_cols = lax.dynamic_slice_in_dim(run_cols, first_row, window_len, 0)
    window_bonds = lax.dynamic_slice_in_dim(run_bonds, first_row, window_len, 0)
    matrix = build_tile(window_cols, window_bonds, chemical)
    return density_column(matrix, window_len, block_width)


def body(ham_columns, bond_mask, owned_counts, fermi_level):
    reach_len = bond_mask.shape[1]
    slots_here = ham_columns.shape[0]
    group_size = lax.axis_size("sub")
    chemical = fermi_level[0]
    counts_flat = owned_counts.reshape(-1)
    group_index = lax.axis_index("grp")
    member_index = lax.axis_index("sub")
    device_index = group_index * group_size + member_index
    my_count = counts_flat[device_index]
    slot_range = jnp.arange(slots_here, dtype=jnp.int32)
    in_use = slot_range < my_count
    gathered_cols, gathered_bonds = (
        lax.all_gather(ham_columns, "sub", axis=0, tiled=True),
        lax.all_gather(bond_mask, "sub", axis=0, tiled=True),
    )
    group_counts = lax.dynamic_index_in_dim(owned_counts, group_index, 0, keepdims=False)
    group_ends = jnp.cumsum(group_counts)
    group_starts = group_ends - group_counts
    group_cols = COLS_MEAN * group_size
    positions = jnp.arange(group_cols, dtype=jnp.int32)
    owner_index = jnp.sum((group_ends[None, :] <= positions[:, None]).astype(jnp.int32), axis=1)
    gather_index = owner_index * slots_here + positions - group_starts[owner_index]
    local_cols = jnp.take(gathered_cols, gather_index, axis=0)
    local_bonds = jnp.take(gathered_bonds, gather_index, axis=0)
    edge_cols, edge_bonds = (
        extended(local_cols, (("grp", 0),), reach_len),
        extended(local_bonds, (("grp", 0),), reach_len),
    )
    first_rows = member_index * COLS_MEAN + jnp.arange(COLS_MEAN, dtype=jnp.int32)
    results = lax.map(
        lambda first_row: window_result(edge_cols, edge_bonds, first_row, chemical), first_rows
    )
    partner_results = partner(results, "sub", 0)
    is_odd = member_index % 2
    lower_first = jnp.concatenate([results, partner_results], axis=0)
    upper_first = jnp.concatenate([partner_results, results], axis=0)
    pair_results = jnp.where(is_odd == 0, lower_first, upper_first)
    pair_start = (member_index - is_odd) * COLS_MEAN
    wanted = jnp.minimum(group_starts[member_index] - pair_start + slot_range, 2 * COLS_MEAN - 1)
    picked = jnp.take(pair_results, wanted, axis=0)
    return jnp.where(in_use[:, None, None, None], picked, jnp.zeros_like(picked))


def solution(mesh):
    placed = (P(("grp", "sub"), None, None, None), P(("grp", "sub"), None), P(), P())
    return jax.shard_map(
        body,
        mesh=mesh,
        in_specs=placed,
        out_specs=P(("grp", "sub"), None, None, None),
        check_vma=False,
    )
```

profile of v0, /device:TPU:1, one launch (start us, length us, event | category | flops | bytes accessed | tf_op | source)
XLA Modules:
  0.0 367.3 jit_solution(13713588425739931471)
XLA Ops:
  8.3 14.4 %all-gather = s32[8,3,4]{2,1,0:T(4,128)S(1)} all-gather(s32[1,3,4]{2,1,0:T(4,128)} %bitcast.405), channel_id=1, replica_groups=mesh['grp'=32,'sub'=8] {'sub'}, dimensions={0}, use_global_device_ids=true | all-gather | bytes 432 | tf_op jit(solution)/shard_map/all_gather | solution.py:116
  24.2 22.8 %all-gather.3.cloned.1.call-done = bf16[24,5,128,128]{3,2,1,0:T(8,128)(2,1)} async-done(((bf16[3,5,128,128]{3,2,1,0:T(8,128)(2,1)}), bf16[24,5,128,128]{3,2,1,0:T(8,128)(2,1)}) %all-gather.3.cloned.1.call-update) | async-done | bytes 3932176 | tf_op jit(solution)/shard_map/all_gather | solution.py:115
  46.9 4.5 %gather_fusion.1 = bf16[16,5,128,128]{3,2,1,0:T(8,128)(2,1)} fusion(bf16[24,5,128,128]{3,2,1,0:T(8,128)(2,1)} %all-gather.3.cloned.1.call-done, s32[1024]{0:T(1024)S(1)} %pad_clamp_fusion.1), kind=kCustom, calls=%fused_computation.1 | custom fusion | bytes 5242944 | tf_op jit(solution)/shard_map/jit(_take)/gather | solution.py:125
  51.4 2.1 broadcast_select_fusion
  54.5 5.2 %collective-permute-start.1 = (bf16[4,5,128,128]{3,2,1,0:T(8,128)(2,1)}, bf16[4,5,128,128]{3,2,1,0:T(8,128)(2,1)}, u32[]{:S(2)}, u32[]{:S(2)}) collective-permute-start(bf16[4,5,128,128]{3,2,1,0:T(8,128)(2,1)} %get-tuple-element.119), channel_id=1, source_target_pairs={{8,0},{16,8},{24,16},{32,24},{40,32},{48,40},{56,48},{64,56},{72,6... | collective-permute-start | bytes 1966088 | tf_op jit(solution)/shard_map/ppermute | solution.py:20
  59.7 4.8 %collective-permute-start.3 = (s32[4,4]{1,0:T(4,128)S(1)}, s32[4,4]{1,0:T(4,128)S(1)}, u32[]{:S(2)}, u32[]{:S(2)}) collective-permute-start(s32[4,4]{1,0:T(4,128)S(1)} %get-tuple-element.121), channel_id=1, source_target_pairs={{8,0},{16,8},{24,16},{32,24},{40,32},{48,40},{56,48},{64,56},{72,6... | collective-permute-start | bytes 200 | tf_op jit(solution)/shard_map/ppermute | solution.py:20
  64.6 9.2 %collective-permute-done.3 = s32[4,4]{1,0:T(4,128)S(1)} collective-permute-done((s32[4,4]{1,0:T(4,128)S(1)}, s32[4,4]{1,0:T(4,128)S(1)}, u32[]{:S(2)}, u32[]{:S(2)}) %collective-permute-start.3) | collective-permute-done | bytes 96 | tf_op jit(solution)/shard_map/ppermute | solution.py:20
  73.8 5.0 %collective-permute-done.2 = s32[4,4]{1,0:T(4,128)S(1)} collective-permute-done((s32[4,4]{1,0:T(4,128)S(1)}, s32[4,4]{1,0:T(4,128)S(1)}, u32[]{:S(2)}, u32[]{:S(2)}) %collective-permute-start.2) | collective-permute-done | bytes 96 | tf_op jit(solution)/shard_map/ppermute | solution.py:19
  79.0 3.3 pad_maximum_fusion
  82.3 270.8 %while.10 = (s32[]{:T(128)}, bf16[2,9,128,128]{3,2,1,0:T(8,128)(2,1)}, s32[2]{0:T(128)S(1)}, bf16[24,5,128,128]{3,2,1,0:T(8,128)(2,1)}, f32[]{:T(128)}, /*index=...) while((s32[]{:T(128)}, ...), condition=%wide.region_3.4_spmd, body=%wide.region_2.3_spmd.sunk | while | flops 2726674432 | bytes 48746780 | solution.py:132
  86.9 2.1 constant_dynamic-update-slice_fusion.81
  110.8 1.4 constant_dynamic-update-slice_fusion.86
  112.2 2.1 fusion.119
  122.4 2.0 constant_dynamic-update-slice_fusion.90
  125.8 2.0 fusion.120
  158.8 1.4 constant_dynamic-update-slice_fusion.109
  161.6 1.4 bitcast_dynamic-update-slice_fusion.48
  164.4 2.1 fusion.122
  174.7 1.4 bitcast_dynamic-update-slice_fusion.54
  179.7 2.1 fusion.124
  186.7 1.4 bitcast_dynamic-update-slice_fusion.58
  189.5 2.1 fusion.126
  195.2 1.4 bitcast_dynamic-update-slice_fusion.61
  198.0 2.1 fusion.128
  200.0 2.9 multiply_convert_fusion.2
  203.6 3.3 fusion.130
  206.9 1.9 fusion.131
  209.7 3.3 fusion.132
  213.0 3.9 %fusion.133 = bf16[1152,128]{1,0:T(8,128)(2,1)S(1)} fusion(bf16[1152,1152]{1,0:T(8,128)(2,1)S(1)} %multiply_convert_fusion.2, f32[512,128]{1,0:T(8,128)S(1)} %broadcast.398, f32[128,128]{1,0:T(8,128)} %fusion.129, f32[1152,128]{1,0:T(8,128)} %fusion.132, f32[1152,128]{1,0:T(8,128)} %fusion.130), kind=kOutput, calls=%fused_computation.16.clone.1 | convolution fusion | flops 681394176 | bytes 4456448 | tf_op jit(solution)/shard_map/while/body/eval_jaxpr/dot_general | solution.py:71
  222.3 2.1 constant_dynamic-update-slice_fusion.81
  246.2 1.4 constant_dynamic-update-slice_fusion.86
  247.7 2.1 fusion.119
  257.8 2.0 constant_dynamic-update-slice_fusion.90
  261.3 2.0 fusion.120
  294.2 1.4 constant_dynamic-update-slice_fusion.109
  299.8 2.1 fusion.122
  310.2 1.4 bitcast_dynamic-update-slice_fusion.54
  315.1 2.1 fusion.124
  322.1 1.4 bitcast_dynamic-update-slice_fusion.58
  324.9 2.1 fusion.126
  330.6 1.4 bitcast_dynamic-update-slice_fusion.61
  333.4 2.1 fusion.128
  335.5 2.9 multiply_convert_fusion.2
  339.0 3.3 fusion.130
  342.3 1.9 fusion.131
  345.1 3.3 fusion.132
  348.4 3.9 %fusion.133 = bf16[1152,128]{1,0:T(8,128)(2,1)S(1)} fusion(bf16[1152,1152]{1,0:T(8,128)(2,1)S(1)} %multiply_convert_fusion.2, f32[512,128]{1,0:T(8,128)S(1)} %broadcast.398, f32[128,128]{1,0:T(8,128)} %fusion.129, f32[1152,128]{1,0:T(8,128)} %fusion.132, f32[1152,128]{1,0:T(8,128)} %fusion.130), kind=kOutput, calls=%fused_computation.16.clone.1 | convolution fusion | flops 681394176 | bytes 4456448 | tf_op jit(solution)/shard_map/while/body/eval_jaxpr/dot_general | solution.py:71
  357.2 1.5 maximum_select_fusion
  (237 shorter events, 108.6 us)
Async XLA Ops:
  6.5 40.4 %all-gather.3.cloned.1.call-start = ((), (), s32[]{:S(2)}) async-start(), calls=%async_computation | async-start | bytes 4423680 | tf_op jit(solution)/shard_map/all_gather | solution.py:115
  54.5 24.5 %collective-permute-start.1 = (bf16[4,5,128,128]{3,2,1,0:T(8,128)(2,1)}, bf16[4,5,128,128]{3,2,1,0:T(8,128)(2,1)}, u32[]{:S(2)}, u32[]{:S(2)}) collective-permute-start(bf16[4,5,128,128]{3,2,1,0:T(8,128)(2,1)} %get-tuple-element.119), channel_id=1, source_target_pairs={{8,0},{16,8},{24,16},{32,24},{40,32},{48,40},{56,48},{64,56},{72,6... | collective-permute-start | bytes 1966088 | tf_op jit(solution)/shard_map/ppermute | solution.py:20
  59.6 19.4 %collective-permute-start = (bf16[4,5,128,128]{3,2,1,0:T(8,128)(2,1)S(1)}, bf16[4,5,128,128]{3,2,1,0:T(8,128)(2,1)}, u32[]{:S(2)}, u32[]{:S(2)}) collective-permute-start(bf16[4,5,128,128]{3,2,1,0:T(8,128)(2,1)S(1)} %get-tuple-element.118), channel_id=1, source_target_pairs={{0,8},{8,16},{16,24},{24,32},{32,40},{40,48},{48,56},{56,64},{64,7... | collective-permute-start | bytes 1966088 | tf_op jit(solution)/shard_map/ppermute | solution.py:19
  59.7 14.1 %collective-permute-start.3 = (s32[4,4]{1,0:T(4,128)S(1)}, s32[4,4]{1,0:T(4,128)S(1)}, u32[]{:S(2)}, u32[]{:S(2)}) collective-permute-start(s32[4,4]{1,0:T(4,128)S(1)} %get-tuple-element.121), channel_id=1, source_target_pairs={{8,0},{16,8},{24,16},{32,24},{40,32},{48,40},{56,48},{64,56},{72,6... | collective-permute-start | bytes 200 | tf_op jit(solution)/shard_map/ppermute | solution.py:20
  64.5 14.3 %collective-permute-start.2 = (s32[4,4]{1,0:T(4,128)S(1)}, s32[4,4]{1,0:T(4,128)S(1)}, u32[]{:S(2)}, u32[]{:S(2)}) collective-permute-start(s32[4,4]{1,0:T(4,128)S(1)} %get-tuple-element.120), channel_id=1, source_target_pairs={{0,8},{8,16},{16,24},{24,32},{32,40},{40,48},{48,56},{56,64},{64,7... | collective-permute-start | bytes 200 | tf_op jit(solution)/shard_map/ppermute | solution.py:19
  82.3 272.2 %copy-start = (s32[32,8]{0,1:T(8,128)S(1)}, s32[32,8]{0,1:T(8,128)}, u32[]{:S(2)}) copy-start(s32[32,8]{0,1:T(8,128)} %param.8) | copy-start | bytes 3076
  353.1 4.1 %collective-permute-start.4 = (bf16[2,9,128,128]{3,2,1,0:T(8,128)(2,1)}, bf16[2,9,128,128]{3,2,1,0:T(8,128)(2,1)S(1)}, u32[]{:S(2)}, u32[]{:S(2)}) collective-permute-start(bf16[2,9,128,128]{3,2,1,0:T(8,128)(2,1)} %get-tuple-element.37), channel_id=1, source_target_pairs={{0,1},{1,0},{2,3},{3,2},{4,5},{5,4},{6,7},{7,6},{8,9},{9,8},{10,11... | collective-permute-start | bytes 1769480 | tf_op jit(solution)/shard_map/ppermute | solution.py:28
Sparse Core Ops, SparseCore 0:
  9.2 37.7 all-gather.2
where the time goes:
time: 374 us; the launch traced here: 367 us
  other arithmetic  116 us (31%)
  loops' own time  92.8 us (25%)
  local copies, waits for them, and re-layouts  54.5 us (15%)
  waiting for transfers between devices  37.6 us (10%)
  matrix products  26.7 us (7%)
  blocking collectives  14.4 us (4%)
  between operations  14.1 us (4%)
  starting transfers between devices  11.4 us (3%)
    another operation x1, loops' own time, body(): lax.map(lambda first_row: window_result(edge_cols, edge_bonds, first_row,...  92.8 us
    while x84, other arithmetic  90.3 us
    while x72, local copies, waits for them, and re-layouts  33.7 us
    dot_general x10, matrix products, product(): jnp.dot(matrix, vector.astype(jnp.bfloat16), preferred_element_type=jnp.f...  26.7 us
    all_gather x1, waiting for transfers between devices, body(): lax.all_gather(ham_columns, 'sub', axis=0, tiled=True)  22.8 us
    all_gather x1, blocking collectives, body(): lax.all_gather(bond_mask, 'sub', axis=0, tiled=True)  14.4 us
    ppermute x2, starting transfers between devices, extended(): after = lax.ppermute(leading, axis, down)  9.97 us
    ppermute x2, waiting for transfers between devices, extended(): after = lax.ppermute(leading, axis, down)  9.16 us
  transfers between devices with their start and end apart: 6, of which 3 were waited for; matrix products, arithmetic and copies ran while one was open for 1% of the time, Pallas kernels for 0%

commit v1 on v0

v1 whole, which is shorter than its diff:
```python
import jax
import jax.numpy as jnp
from jax import lax
from jax.experimental import pallas as pl
from jax.experimental.pallas import tpu as pltpu
from jax.sharding import PartitionSpec as P

AXES = ("grp", "sub")
CHIP_COLS = 4
BF16 = jnp.bfloat16
F32 = jnp.float32


def place(counts_ref):
    group = lax.axis_index("grp")
    member = lax.axis_index("sub")
    parity = member % 2
    low_count = counts_ref[group, member - parity]
    first = jnp.where(parity == 0, 0, low_count)
    return parity, low_count, first, counts_ref[group, member]


def pack_kernel(counts_ref, bond_ref, mate_bond_ref, ham_ref, mate_ref, up_ref, down_ref):
    parity, low_count, _, _ = place(counts_ref)

    def source(t):
        in_low = t < low_count
        slot = jnp.where(in_low, t, t - low_count)
        return in_low == (parity == 0), slot

    def block(t, o, target, row):
        mine, slot = source(t)

        def put(cols, bonds):
            value = cols[slot, o]
            if o:
                value = value * (bonds[slot, o - 1] != 0).astype(F32).astype(BF16)
            target[row : row + 128, :] = value

        pl.when(mine)(lambda: put(ham_ref, bond_ref))
        pl.when(jnp.logical_not(mine))(lambda: put(mate_ref, mate_bond_ref))

    for h in range(2):
        for o in range(5):
            block(parity * 2 + h, o, up_ref, (h * 5 + o) * 128)
    rows = []
    for t in range(CHIP_COLS):
        mine, slot = source(t)
        for o in range(4):
            bit = jnp.where(mine, bond_ref[slot, o], mate_bond_ref[slot, o])
            rows.append(jnp.full((1, 128), bit.astype(F32)))
    up_ref[1280:1296, :] = jnp.concatenate(rows, axis=0).astype(BF16)

    @pl.when(parity == 0)
    def _():
        for k, (t, o) in enumerate([(0, 0), (0, 1), (0, 2), (0, 3), (3, 0)]):
            block(t, o, down_ref, k * 128)

    @pl.when(parity == 1)
    def _():
        for k, (t, o) in enumerate([(1, 0), (1, 1), (1, 2), (2, 0), (2, 1)]):
            block(t, o, down_ref, k * 128)


def main_kernel(
    counts_ref, bond_ref, mate_bond_ref, mu_ref, ham_hbm, mate_hbm, up_hbm, mate_up_hbm, down_hbm, mate_down_hbm,
    out_hbm, cols, bits_in, bits, x, first, kept, va, vb, mask, out, sems, out_sems,
):
    parity, low_count, base, count = place(counts_ref)

    copies = []
    for t in range(CHIP_COLS):
        in_low = t < low_count
        slot = jnp.where(in_low, t, t - low_count)
        mine = in_low == (parity == 0)
        own = pltpu.make_async_copy(ham_hbm.at[slot], cols.at[4 + t], sems.at[t])
        mate = pltpu.make_async_copy(mate_hbm.at[slot], cols.at[4 + t], sems.at[t])
        pl.when(mine)(own.start)
        pl.when(jnp.logical_not(mine))(mate.start)
        copies.append(own)
    for k, (ref, half) in enumerate([(up_hbm, parity), (mate_up_hbm, 1 - parity)]):
        for h in range(2):
            for o in range(5):
                c = pltpu.make_async_copy(
                    ref.at[pl.ds((h * 5 + o) * 128, 128)], cols.at[half * 2 + h, o], sems.at[5 + k * 10 + h * 5 + o]
                )
                c.start()
                copies.append(c)
    c = pltpu.make_async_copy(up_hbm.at[pl.ds(1280, 16)], bits_in, sems.at[4])
    c.start()
    copies.append(c)
    low_list = [(8, 0), (8, 1), (8, 2), (8, 3), (11, 0)]
    high_list = [(9, 0), (9, 1), (9, 2), (10, 0), (10, 1)]
    for k in range(5):
        for n, ref in enumerate([down_hbm, mate_down_hbm]):
            is_low = parity == n
            p = jnp.where(is_low, low_list[k][0], high_list[k][0])
            o = jnp.where(is_low, low_list[k][1], high_list[k][1])
            c = pltpu.make_async_copy(ref.at[pl.ds(k * 128, 128)], cols.at[p, o], sems.at[25 + k * 2 + n])
            c.start()
            copies.append(c)

    zero = jnp.zeros((128, 128), BF16)
    for i in range(12):
        for j in range(12):
            if abs(i - j) > 4 or i == 11 or j == 11:
                x[i * 128 : (i + 1) * 128, j * 128 : (j + 1) * 128] = zero
    bits[32:64, :] = jnp.zeros((32, 128), F32)
    for t in range(CHIP_COLS):
        in_low = t < low_count
        slot = jnp.where(in_low, t, t - low_count)
        mine = in_low == (parity == 0)
        for o in range(4):
            bit = jnp.where(mine, bond_ref[slot, o], mate_bond_ref[slot, o]).astype(F32)
            bits[16 + t * 4 + o : 17 + t * 4 + o, :] = jnp.full((1, 128), bit)
    for c in copies:
        c.wait()
    bits[0:16, :] = bits_in[...].astype(F32)

    one = jnp.ones((1, 128), F32)
    for i in range(3):
        c = 4 + i
        for u in range(12):
            if u == c:
                row = one
            elif c < u <= c + 4:
                row = bits[pl.ds((c + base) * 4 + (u - c - 1), 1), :]
            elif c - 4 <= u < c:
                row = bits[pl.ds((u + base) * 4 + (c - u - 1), 1), :]
            else:
                row = jnp.zeros((1, 128), F32)
            mask[i : i + 1, u * 128 : (u + 1) * 128] = row

    mu = mu_ref[0]
    eye = (
        lax.broadcasted_iota(jnp.int32, (128, 128), 0) == lax.broadcasted_iota(jnp.int32, (128, 128), 1)
    ).astype(F32)
    for u in range(11):
        p = u + base
        pc = jnp.minimum(p, 11)
        d = (cols[pc, 0].astype(F32) - mu * eye) * 0.25
        d = jnp.where(p <= 11, d, 0.0)
        x[u * 128 : (u + 1) * 128, u * 128 : (u + 1) * 128] = d.astype(BF16)
        for o in range(1, 5):
            v = u + o
            if v > 10:
                continue
            row = jnp.where(jnp.logical_and(p >= 4, p < 8), bits[pl.ds(p * 4 + o - 1, 1), :], one * 1.0)
            blk = jnp.where(p + o <= 11, cols[pc, o].astype(F32) * (row * 0.25), 0.0)
            x[v * 128 : (v + 1) * 128, u * 128 : (u + 1) * 128] = blk.astype(BF16)
            x[u * 128 : (u + 1) * 128, v * 128 : (v + 1) * 128] = blk.T.astype(BF16)

    def product(src, n, r0, r1, off=0):
        k0, k1 = max(0, n - 2), min(6, n + 3)
        acc = jnp.dot(
            src[off + r0 : off + r1, k0 * 256 : k1 * 256],
            x[k0 * 256 : k1 * 256, n * 256 : (n + 1) * 256],
            preferred_element_type=F32,
        )
        parts = []
        for i in range(r0 // 128, r1 // 128):
            m = mask[i : i + 1, n * 256 : (n + 1) * 256]
            parts.append(acc[i * 128 - r0 : (i + 1) * 128 - r0, :] * m)
        return parts

    span = [(0, 256), (0, 384), (0, 384), (0, 384), (0, 384), (256, 384)]

    def zero_rest(ref):
        ref[256:384, 0:256] = jnp.zeros((128, 256), ref.dtype)
        ref[0:256, 1280:1536] = jnp.zeros((256, 256), ref.dtype)

    zero_rest(va)
    zero_rest(vb)

    def sweep(src, off, use):
        for n in range(6):
            r0, r1 = span[n]
            parts = product(src, n, r0, r1, off)
            for i, part in zip(range(r0 // 128, r1 // 128), parts):
                use(i, n, part)

    def sl(i, n):
        return (slice(i * 128, (i + 1) * 128), slice(n * 256, (n + 1) * 256))

    def store(ref):
        def use(i, n, part):
            ref[sl(i, n)] = part.astype(BF16)

        return use

    sweep(x, 512, store(va))

    def end_one(i, n, part):
        rows = slice(512 + i * 128, 512 + (i + 1) * 128)
        s = 1.5 * x[rows, n * 256 : (n + 1) * 256].astype(F32) - 0.5 * part
        kept[sl(i, n)] = s
        vb[sl(i, n)] = s.astype(BF16)

    sweep(va, 0, end_one)

    def keep_first(ref):
        def use(i, n, part):
            first[sl(i, n)] = part
            ref[sl(i, n)] = part.astype(BF16)

        return use

    sweep(vb, 0, keep_first(va))
    sweep(va, 0, store(vb))

    def end_two(i, n, part):
        va[sl(i, n)] = (1.5 * first[sl(i, n)] - 0.5 * part).astype(BF16)

    sweep(vb, 0, end_two)
    sweep(va, 0, keep_first(vb))
    sweep(vb, 0, store(va))

    def end_three(i, n, part):
        s3 = 1.5 * first[sl(i, n)] - 0.5 * part
        y = 1.5 * kept[sl(i, n)] - 0.5 * s3
        for h in range(2):
            w = 2 * n + h - i
            if 0 <= w < 9:
                d = -0.5 * y[:, h * 128 : (h + 1) * 128]
                if w == 4:
                    d = d + 0.5 * eye
                d = jnp.where(i < count, d, 0.0)
                out[i, w] = d.T.astype(BF16)

    sweep(va, 0, end_three)
    c = pltpu.make_async_copy(out, out_hbm, out_sems.at[0])
    c.start()
    c.wait()


def shift(value, step):
    size = lax.axis_size("grp") * lax.axis_size("sub")
    return lax.ppermute(value, AXES, [(s, (s + step) % size) for s in range(size)])


def mate_of(value):
    return lax.ppermute(value, "sub", [(s, s ^ 1) for s in range(lax.axis_size("sub"))])


def body(ham_columns, bond_mask, owned_counts, fermi_level):
    smem = pl.BlockSpec(memory_space=pltpu.SMEM)
    vmem = pl.BlockSpec(memory_space=pltpu.VMEM)
    hbm = pl.BlockSpec(memory_space=pltpu.HBM)
    mate_bond = mate_of(bond_mask)
    mate_ham = mate_of(ham_columns)
    up, down = pl.pallas_call(
        pack_kernel,
        out_shape=(jax.ShapeDtypeStruct((1296, 128), BF16), jax.ShapeDtypeStruct((640, 128), BF16)),
        in_specs=[smem, smem, smem, vmem, vmem],
        out_specs=(vmem, vmem),
        name="pack",
    )(owned_counts, bond_mask, mate_bond, ham_columns, mate_ham)
    up_got = shift(up, 2)
    down_got = shift(down, -2)
    mate_down = mate_of(down_got)
    mate_up = mate_of(up_got)
    return pl.pallas_call(
        main_kernel,
        out_shape=jax.ShapeDtypeStruct((3, 9, 128, 128), BF16),
        in_specs=[smem, smem, smem, smem] + [hbm] * 6,
        out_specs=hbm,
        scratch_shapes=[
            pltpu.VMEM((12, 5, 128, 128), BF16),
            pltpu.VMEM((16, 128), BF16),
            pltpu.VMEM((64, 128), F32),
            pltpu.VMEM((1536, 1536), BF16),
            pltpu.VMEM((384, 1536), F32),
            pltpu.VMEM((384, 1536), F32),
            pltpu.VMEM((384, 1536), BF16),
            pltpu.VMEM((384, 1536), BF16),
            pltpu.VMEM((8, 1536), F32),
            pltpu.VMEM((3, 9, 128, 128), BF16),
            pltpu.SemaphoreType.DMA((35,)),
            pltpu.SemaphoreType.DMA((1,)),
        ],
        name="columns",
    )(owned_counts, bond_mask, mate_bond, fermi_level, ham_columns, mate_ham, up_got, mate_up, down_got, mate_down)


def solution(mesh):
    placed = (P(AXES, None, None, None), P(AXES, None), P(), P())
    return jax.shard_map(
        body,
        mesh=mesh,
        in_specs=placed,
        out_specs=P(AXES, None, None, None),
        check_vma=False,
    )
```

time: 374 us -> 48.3 us (0.13); the launches traced: 367 us -> 48.1 us
  other arithmetic: 116 us -> 0 us
  loops' own time: 92.8 us -> 0 us
  local copies, waits for them, and re-layouts: 54.5 us -> 4.12 us
  matrix products: 26.7 us -> 0 us
  waiting for transfers between devices: 37.6 us -> 21.8 us
  Pallas kernels: 0 us -> 14.9 us
  blocking collectives: 14.4 us -> 0 us
  between operations: 14.1 us -> 0.83 us
  starting transfers between devices: 11.4 us -> 6.47 us
    another operation x1 -> x0, loops' own time: 92.8 us -> none  [body(): lax.map(lambda first_row: window_result(edge_cols, edge_bonds, first_row,...]
    while x84 -> x0, other arithmetic: 90.3 us -> none
    while x72 -> x0, local copies, waits for them, and re-layouts: 33.7 us -> none
    dot_general x10 -> x0, matrix products: 26.7 us -> none  [product(): jnp.dot(matrix, vector.astype(jnp.bfloat16), preferred_element_type=jnp.f...]
    all_gather x1 -> x0, waiting for transfers between devices: 22.8 us -> none  [body(): lax.all_gather(ham_columns, 'sub', axis=0, tiled=True)]
    pallas_call x0 -> x2, Pallas kernels: none -> 14.9 us  [the longest x1 12.7 us: body(): pl.pallas_call(main_kernel, out_shape=jax.ShapeDtypeStruct((3, 9, 128, 12...]
    all_gather x1 -> x0, blocking collectives: 14.4 us -> none  [body(): lax.all_gather(bond_mask, 'sub', axis=0, tiled=True)]
    concatenate x6 -> x0, other arithmetic: 9.04 us -> none  [the longest x2 4.11 us: build_tile(): jnp.concatenate(rows_list, axis=0) / spectral_span]
  transfers between devices with their start and end apart: 6 -> 6, of which waited for: 3 -> 4; matrix products, arithmetic and copies ran while one was open for 1% -> 3% of each run, Pallas kernels for 0% -> 0%
where the time goes in v1:
time: 48.3 us; the launch traced here: 48.1 us
  waiting for transfers between devices  21.8 us (45%)
  Pallas kernels  14.9 us (31%)
  starting transfers between devices  6.47 us (13%)
  local copies, waits for them, and re-layouts  4.12 us (9%)
  between operations  0.83 us (2%)
    ppermute x2, waiting for transfers between devices, shift(): lax.ppermute(value, AXES, [(s, (s + step) % size) for s in range(size)])  21 us
    pallas_call x1, Pallas kernels, body(): pl.pallas_call(main_kernel, out_shape=jax.ShapeDtypeStruct((3, 9, 128, 12...  12.7 us
    ppermute x4, starting transfers between devices, mate_of(): lax.ppermute(value, 'sub', [(s, s ^ 1) for s in range(lax.axis_size('sub'...  5.01 us
    unnamed x13, local copies, waits for them, and re-layouts  4.12 us
    pallas_call x1, Pallas kernels, body(): pl.pallas_call(pack_kernel, out_shape=(jax.ShapeDtypeStruct((1296, 128),...  2.15 us
    ppermute x2, starting transfers between devices, shift(): lax.ppermute(value, AXES, [(s, (s + step) % size) for s in range(size)])  1.47 us
  transfers between devices with their start and end apart: 6, of which 4 were waited for; matrix products, arithmetic and copies ran while one was open for 3% of the time, Pallas kernels for 0%

profile of v1, /device:TPU:1, one launch (start us, length us, event | category | flops | bytes accessed | tf_op | source)
XLA Modules:
  0.0 48.1 jit_solution(15514660038957185955)
XLA Ops:
  0.0 3.2 %collective-permute-start.1 = (bf16[3,5,128,128]{3,2,1,0:T(8,128)(2,1)}, bf16[3,5,128,128]{3,2,1,0:T(8,128)(2,1)S(1)}, u32[]{:S(2)}, u32[]{:S(2)}) collective-permute-start(bf16[3,5,128,128]{3,2,1,0:T(8,128)(2,1)} %ham_hbm.1), channel_id=1, source_target_pairs={{0,1},{1,0},{2,3},{3,2},{4,5},{5,4},{6,7},{7,6},{8,9},{9,8},{10,11... | collective-permute-start | bytes 1474568 | tf_op jit(solution)/shard_map/ppermute | solution.py:242
  3.2 0.0 collective-permute-start
  3.2 1.4 %copy.6.counts_ref = s32[32,8]{1,0:T(8,128)} copy(s32[32,8]{0,1:T(8,128)} %param.6) | data formatting | bytes 2048 | tf_op args[2]
  4.6 0.3 collective-permute-done.mate_bond_ref
  4.9 0.0 copy-start.5
  4.9 0.0 collective-permute-done.1.mate_ref.mate_hbm
  4.9 0.6 %copy-done.5 = s32[3,4]{1,0:T(4,128)} copy-done((s32[3,4]{1,0:T(4,128)}, s32[3,4]{1,0:T(4,128)S(1)}, u32[]{:S(2)}) %copy-start.5) | copy-done | bytes 72
  5.5 0.0 copy-start
  5.5 0.8 %copy-done = bf16[3,5,128,128]{3,2,1,0:T(8,128)(2,1)} copy-done((bf16[3,5,128,128]{3,2,1,0:T(8,128)(2,1)}, bf16[3,5,128,128]{3,2,1,0:T(8,128)(2,1)S(1)}, u32[]{:S(2)}) %copy-start) | copy-done | bytes 491544
  6.3 2.2 %pack.1 = (bf16[1296,128]{1,0:T(8,128)(2,1)}, bf16[640,128]{1,0:T(8,128)(2,1)}) custom-call(s32[32,8]{1,0:T(8,128)} %copy.6.counts_ref, s32[3,4]{1,0:T(4,128)} %bond_ref.3, s32[3,4]{1,0:T(4,128)} %copy-done.5, bf16[3,5,128,128]{3,2,1,0:T(8,128)(2,1)} %ham_hbm.1, bf16[3,5,128,128]{3,2,1,0:T(8,128)(2,1)} %copy-done), custom_call_target="tpu_custom_call" | custom-call | tf_op jit(solution)/shard_map/pack/pallas_call | solution.py:251
  8.4 0.0 collective-permute-start.2
  8.4 16.5 %collective-permute-done.2.up_hbm = bf16[1296,128]{1,0:T(8,128)(2,1)S(1)} collective-permute-done((bf16[1296,128]{1,0:T(8,128)(2,1)}, bf16[1296,128]{1,0:T(8,128)(2,1)S(1)}, u32[]{:S(2)}, u32[]{:S(2)}) %collective-permute-start.2) | collective-permute-done | bytes 331808 | tf_op jit(solution)/shard_map/ppermute | solution.py:238
  25.0 0.0 copy-start.1
  25.0 0.9 %collective-permute-start.3 = (bf16[1296,128]{1,0:T(8,128)(2,1)S(1)}, bf16[1296,128]{1,0:T(8,128)(2,1)S(1)}, u32[]{:S(2)}, u32[]{:S(2)}) collective-permute-start(bf16[1296,128]{1,0:T(8,128)(2,1)S(1)} %collective-permute-done.2.up_hbm), channel_id=1, source_target_pairs={{0,1},{1,0},{2,3},{3,2},{4,5},{5,4},{6,7},{7,6},{8,9},{9,8},{10,11... | collective-permute-start | bytes 995336 | tf_op jit(solution)/shard_map/ppermute | solution.py:242
  25.9 1.5 %collective-permute-start.4 = (bf16[640,128]{1,0:T(8,128)(2,1)}, bf16[640,128]{1,0:T(8,128)(2,1)S(1)}, u32[]{:S(2)}, u32[]{:S(2)}) collective-permute-start(bf16[640,128]{1,0:T(8,128)(2,1)} %get-tuple-element.8), channel_id=1, source_target_pairs={{0,254},{1,255},{2,0},{3,1},{4,2},{5,3},{6,4},{7,5},{8,6},{9,7},{1... | collective-permute-start | bytes 491528 | tf_op jit(solution)/shard_map/ppermute | solution.py:238
  27.4 4.5 %collective-permute-done.4.down_hbm = bf16[640,128]{1,0:T(8,128)(2,1)S(1)} collective-permute-done((bf16[640,128]{1,0:T(8,128)(2,1)}, bf16[640,128]{1,0:T(8,128)(2,1)S(1)}, u32[]{:S(2)}, u32[]{:S(2)}) %collective-permute-start.4) | collective-permute-done | bytes 163872 | tf_op jit(solution)/shard_map/ppermute | solution.py:238
  31.9 0.0 copy-start.3
  31.9 0.9 %collective-permute-start.5 = (bf16[640,128]{1,0:T(8,128)(2,1)S(1)}, bf16[640,128]{1,0:T(8,128)(2,1)S(1)}, u32[]{:S(2)}, u32[]{:S(2)}) collective-permute-start(bf16[640,128]{1,0:T(8,128)(2,1)S(1)} %collective-permute-done.4.down_hbm), channel_id=1, source_target_pairs={{0,1},{1,0},{2,3},{3,2},{4,5},{5,4},{6,7},{7,6},{8,9},{9,8},{10,11... | collective-permute-start | bytes 491528 | tf_op jit(solution)/shard_map/ppermute | solution.py:242
  33.4 0.4 collective-permute-done.5.mate_down_hbm
  33.8 0.0 copy-start.4
  33.8 0.0 collective-permute-done.3.mate_up_hbm
  33.8 0.0 copy-done.1
  33.8 0.0 copy-done.3
  33.8 0.6 %copy-done.4 = bf16[640,128]{1,0:T(8,128)(2,1)} copy-done((bf16[640,128]{1,0:T(8,128)(2,1)}, bf16[640,128]{1,0:T(8,128)(2,1)S(1)}, u32[]{:S(2)}) %copy-start.4) | copy-done | bytes 163864
  34.4 0.0 copy-start.2
  34.4 0.7 %copy-done.2 = bf16[1296,128]{1,0:T(8,128)(2,1)} copy-done((bf16[1296,128]{1,0:T(8,128)(2,1)}, bf16[1296,128]{1,0:T(8,128)(2,1)S(1)}, u32[]{:S(2)}) %copy-start.2) | copy-done | bytes 331800
  35.2 12.7 %columns.1 = bf16[3,9,128,128]{3,2,1,0:T(8,128)(2,1)} custom-call(s32[32,8]{1,0:T(8,128)} %copy.6.counts_ref, s32[3,4]{1,0:T(4,128)} %bond_ref.3, s32[3,4]{1,0:T(4,128)} %copy-done.5, f32[1]{0:T(128)S(6)} %copy.7.mu_ref, bf16[3,5,128,128]{3,2,1,0:T(8,128)(2,1)} %ham_hbm.1, bf16[3,5,128,128]{3,2,1,0:T(8,128)(2,1)} %copy-done, bf16[1296,128]{1,0:T(8,128)(2,1)} %copy-done.1, ...), custom_call_target="tpu_custom_call" | custom-call | tf_op jit(solution)/shard_map/columns/pallas_call | solution.py:262
Async XLA Ops:
  0.0 4.9 %collective-permute-start.1 = (bf16[3,5,128,128]{3,2,1,0:T(8,128)(2,1)}, bf16[3,5,128,128]{3,2,1,0:T(8,128)(2,1)S(1)}, u32[]{:S(2)}, u32[]{:S(2)}) collective-permute-start(bf16[3,5,128,128]{3,2,1,0:T(8,128)(2,1)} %ham_hbm.1), channel_id=1, source_target_pairs={{0,1},{1,0},{2,3},{3,2},{4,5},{5,4},{6,7},{7,6},{8,9},{9,8},{10,11... | collective-permute-start | bytes 1474568 | tf_op jit(solution)/shard_map/ppermute | solution.py:242
  3.2 1.7 %collective-permute-start = (s32[3,4]{1,0:T(4,128)}, s32[3,4]{1,0:T(4,128)S(1)}, u32[]{:S(2)}, u32[]{:S(2)}) collective-permute-start(s32[3,4]{1,0:T(4,128)} %bond_ref.3), channel_id=1, source_target_pairs={{0,1},{1,0},{2,3},{3,2},{4,5},{5,4},{6,7},{7,6},{8,9},{9,8},{10,11... | collective-permute-start | bytes 152 | tf_op jit(solution)/shard_map/ppermute | solution.py:242
  4.9 0.6 %copy-start.5 = (s32[3,4]{1,0:T(4,128)}, s32[3,4]{1,0:T(4,128)S(1)}, u32[]{:S(2)}) copy-start(s32[3,4]{1,0:T(4,128)S(1)} %collective-permute-done.mate_bond_ref) | copy-start | bytes 148
  5.5 0.8 %copy-start = (bf16[3,5,128,128]{3,2,1,0:T(8,128)(2,1)}, bf16[3,5,128,128]{3,2,1,0:T(8,128)(2,1)S(1)}, u32[]{:S(2)}) copy-start(bf16[3,5,128,128]{3,2,1,0:T(8,128)(2,1)S(1)} %collective-permute-done.1.mate_ref.mate_hbm) | copy-start | bytes 1474564
  8.4 16.5 %collective-permute-start.2 = (bf16[1296,128]{1,0:T(8,128)(2,1)}, bf16[1296,128]{1,0:T(8,128)(2,1)S(1)}, u32[]{:S(2)}, u32[]{:S(2)}) collective-permute-start(bf16[1296,128]{1,0:T(8,128)(2,1)} %get-tuple-element.7), channel_id=1, source_target_pairs={{0,2},{1,3},{2,4},{3,5},{4,6},{5,7},{6,8},{7,9},{8,10},{9,11},{10,... | collective-permute-start | bytes 995336 | tf_op jit(solution)/shard_map/ppermute | solution.py:238
  25.0 8.8 %copy-start.1 = (bf16[1296,128]{1,0:T(8,128)(2,1)}, bf16[1296,128]{1,0:T(8,128)(2,1)S(1)}, u32[]{:S(2)}) copy-start(bf16[1296,128]{1,0:T(8,128)(2,1)S(1)} %collective-permute-done.2.up_hbm) | copy-start | bytes 995332
  25.0 8.8 %collective-permute-start.3 = (bf16[1296,128]{1,0:T(8,128)(2,1)S(1)}, bf16[1296,128]{1,0:T(8,128)(2,1)S(1)}, u32[]{:S(2)}, u32[]{:S(2)}) collective-permute-start(bf16[1296,128]{1,0:T(8,128)(2,1)S(1)} %collective-permute-done.2.up_hbm), channel_id=1, source_target_pairs={{0,1},{1,0},{2,3},{3,2},{4,5},{5,4},{6,7},{7,6},{8,9},{9,8},{10,11... | collective-permute-start | bytes 995336 | tf_op jit(solution)/shard_map/ppermute | solution.py:242
  25.9 6.0 %collective-permute-start.4 = (bf16[640,128]{1,0:T(8,128)(2,1)}, bf16[640,128]{1,0:T(8,128)(2,1)S(1)}, u32[]{:S(2)}, u32[]{:S(2)}) collective-permute-start(bf16[640,128]{1,0:T(8,128)(2,1)} %get-tuple-element.8), channel_id=1, source_target_pairs={{0,254},{1,255},{2,0},{3,1},{4,2},{5,3},{6,4},{7,5},{8,6},{9,7},{1... | collective-permute-start | bytes 491528 | tf_op jit(solution)/shard_map/ppermute | solution.py:238
  31.9 1.9 %copy-start.3 = (bf16[640,128]{1,0:T(8,128)(2,1)}, bf16[640,128]{1,0:T(8,128)(2,1)S(1)}, u32[]{:S(2)}) copy-start(bf16[640,128]{1,0:T(8,128)(2,1)S(1)} %collective-permute-done.4.down_hbm) | copy-start | bytes 491524
  31.9 1.9 %collective-permute-start.5 = (bf16[640,128]{1,0:T(8,128)(2,1)S(1)}, bf16[640,128]{1,0:T(8,128)(2,1)S(1)}, u32[]{:S(2)}, u32[]{:S(2)}) collective-permute-start(bf16[640,128]{1,0:T(8,128)(2,1)S(1)} %collective-permute-done.4.down_hbm), channel_id=1, source_target_pairs={{0,1},{1,0},{2,3},{3,2},{4,5},{5,4},{6,7},{7,6},{8,9},{9,8},{10,11... | collective-permute-start | bytes 491528 | tf_op jit(solution)/shard_map/ppermute | solution.py:242
  33.8 0.7 %copy-start.4 = (bf16[640,128]{1,0:T(8,128)(2,1)}, bf16[640,128]{1,0:T(8,128)(2,1)S(1)}, u32[]{:S(2)}) copy-start(bf16[640,128]{1,0:T(8,128)(2,1)S(1)} %collective-permute-done.5.mate_down_hbm) | copy-start | bytes 491524
  34.4 0.7 %copy-start.2 = (bf16[1296,128]{1,0:T(8,128)(2,1)}, bf16[1296,128]{1,0:T(8,128)(2,1)S(1)}, u32[]{:S(2)}) copy-start(bf16[1296,128]{1,0:T(8,128)(2,1)S(1)} %collective-permute-done.3.mate_up_hbm) | copy-start | bytes 995332

commit v2 on v1

v2 whole, which is shorter than its diff:
```python
import jax
import jax.numpy as jnp
from jax import lax
from jax.experimental import pallas as pl
from jax.experimental.pallas import tpu as pltpu
from jax.sharding import PartitionSpec as P

AXES = ("grp", "sub")
CHIP_COLS = 4
BF16 = jnp.bfloat16
F32 = jnp.float32

DOWN = (((0, 0), (0, 1), (0, 2), (0, 3), (3, 0)), ((1, 0), (1, 1), (1, 2), (2, 0), (2, 1)))


def place(counts_ref):
    group = lax.axis_index("grp")
    member = lax.axis_index("sub")
    parity = member % 2
    return parity, counts_ref[group, member - parity], counts_ref[group, member]


def pack_kernel(counts_ref, bond_ref, mate_bond_ref, ham_ref, mate_ref, up_ref, down_ref, local_ref, bits_ref):
    parity, low_count, _ = place(counts_ref)
    for t in range(CHIP_COLS):
        in_low = t < low_count
        slot = jnp.where(in_low, t, t - low_count)
        mine = in_low == (parity == 0)
        bonds = jnp.where(mine, bond_ref[pl.ds(slot, 1), :], mate_bond_ref[pl.ds(slot, 1), :]).astype(F32)
        for o in range(5):
            value = jnp.where(mine, ham_ref[slot, o], mate_ref[slot, o])
            if o:
                row = jnp.broadcast_to(bonds[:, o - 1 : o], (1, 128))
                bits_ref[t * 4 + o - 1 : t * 4 + o, :] = row
                value = value * row.astype(BF16)
            local_ref[t * 5 + o] = value
    for k in range(10):
        up_ref[k * 128 : (k + 1) * 128, :] = local_ref[parity * 10 + k]
    up_ref[1280:1296, :] = bits_ref[...].astype(BF16)
    for k in range(5):
        (t, o), (tt, oo) = DOWN[0][k], DOWN[1][k]
        down_ref[k * 128 : (k + 1) * 128, :] = local_ref[jnp.where(parity == 0, t * 5 + o, tt * 5 + oo)]


def main_kernel(
    counts_ref, mu_ref, local_ref, local_bits, up_ref, mate_up_ref, down_ref, mate_down_ref,
    out_hbm, bits, x, first, kept, va, vb, mask, out, out_sems,
):
    parity, _, count = place(counts_ref)
    even = parity == 0

    bits[0:16, :] = up_ref[1280:1296, :].astype(F32)
    bits[16:32, :] = local_bits[...]

    for i in range(3):
        c = 4 + i
        for u in range(12):
            if u == c:
                row = jnp.ones((1, 128), F32)
            elif c < u <= c + 4:
                row = bits[pl.ds((c + parity) * 4 + (u - c - 1), 1), :]
            elif c - 4 <= u < c:
                row = bits[pl.ds((u + parity) * 4 + (c - u - 1), 1), :]
            else:
                row = jnp.zeros((1, 128), F32)
            mask[i : i + 1, u * 128 : (u + 1) * 128] = row

    mu = mu_ref[0]
    eye = (
        lax.broadcasted_iota(jnp.int32, (128, 128), 0) == lax.broadcasted_iota(jnp.int32, (128, 128), 1)
    ).astype(F32)
    zero = jnp.zeros((128, 128), BF16)

    def block(p, o):
        if p < 4:
            rows = slice(((p % 2) * 5 + o) * 128, ((p % 2) * 5 + o + 1) * 128)
            return jnp.where(parity == p // 2, up_ref[rows, :], mate_up_ref[rows, :])
        if p < 8:
            return local_ref[(p - 4) * 5 + o]
        side = 0 if (p - 8, o) in DOWN[0] else 1
        k = DOWN[side].index((p - 8, o))
        rows = slice(k * 128, (k + 1) * 128)
        return jnp.where(parity == side, down_ref[rows, :], mate_down_ref[rows, :])

    def cell(i, j):
        return (slice(i * 128, (i + 1) * 128), slice(j * 128, (j + 1) * 128))

    @pl.when(count > 0)
    def _():
        for p in range(13):
            for q in range(p + 1):
                if p - q > 4 or p == 12:
                    x[cell(p, q)] = zero
                    x[cell(q, p)] = zero
        for p in range(12):
            x[cell(p, p)] = ((block(p, 0).astype(F32) - mu * eye) * 0.25).astype(BF16)
            for o in range(1, 5):
                if p + o < 12:
                    b = block(p, o).astype(F32) * 0.25
                    x[cell(p + o, p)] = b.astype(BF16)
                    x[cell(p, p + o)] = b.T.astype(BF16)

    def at(k):
        return pl.multiple_of(parity * 128 + k, 128)

    span = [(0, 256), (0, 384), (0, 384), (0, 384), (0, 384), (256, 384)]

    def sweep(src, use):
        for n in range(6):
            r0, r1 = span[n]
            k0, k1 = max(0, n - 2), min(6, n + 3)
            acc = jnp.dot(
                src(slice(r0, r1), k0 * 256, k1 * 256),
                x[pl.ds(at(k0 * 256), (k1 - k0) * 256), pl.ds(at(n * 256), 256)],
                preferred_element_type=F32,
            )
            for i in range(r0 // 128, r1 // 128):
                m = mask[i : i + 1, n * 256 : (n + 1) * 256]
                use(i, n, acc[i * 128 - r0 : (i + 1) * 128 - r0, :] * m)

    def of(ref):
        return lambda rows, k0, k1: ref[rows, k0:k1]

    def x_rows(rows, k0, k1):
        return x[pl.ds(at(512 + rows.start), rows.stop - rows.start), pl.ds(at(k0), k1 - k0)]

    for ref in (va, vb):
        ref[256:384, 0:256] = jnp.zeros((128, 256), BF16)
        ref[0:256, 1280:1536] = jnp.zeros((256, 256), BF16)

    def sl(i, n):
        return (slice(i * 128, (i + 1) * 128), slice(n * 256, (n + 1) * 256))

    def store(ref):
        def use(i, n, part):
            ref[sl(i, n)] = part.astype(BF16)

        return use

    pl.when(count > 0)(lambda: sweep(x_rows, store(va)))

    def end_one(i, n, part):
        f = x_rows(slice(i * 128, (i + 1) * 128), n * 256, (n + 1) * 256).astype(F32)
        s = 1.5 * f - 0.5 * part
        kept[sl(i, n)] = s
        vb[sl(i, n)] = s.astype(BF16)

    pl.when(count > 0)(lambda: sweep(of(va), end_one))

    def keep_first(ref):
        def use(i, n, part):
            first[sl(i, n)] = part
            ref[sl(i, n)] = part.astype(BF16)

        return use

    pl.when(count > 0)(lambda: sweep(of(vb), keep_first(va)))
    pl.when(count > 0)(lambda: sweep(of(va), store(vb)))

    def end_two(i, n, part):
        va[sl(i, n)] = (1.5 * first[sl(i, n)] - 0.5 * part).astype(BF16)

    pl.when(count > 0)(lambda: sweep(of(vb), end_two))
    pl.when(count > 0)(lambda: sweep(of(va), keep_first(vb)))
    pl.when(count > 0)(lambda: sweep(of(vb), store(va)))

    turn = jnp.where(jnp.logical_and(parity == 1, count == 1), 1, 0)
    slots = [(i + turn) % 3 for i in range(3)]

    def end_three(i, n, part):
        s3 = 1.5 * first[sl(i, n)] - 0.5 * part
        y = 1.5 * kept[sl(i, n)] - 0.5 * s3
        for h in range(2):
            w = 2 * n + h - i
            if 0 <= w < 9:
                d = -0.5 * y[:, h * 128 : (h + 1) * 128]
                if w == 4:
                    d = d + 0.5 * eye
                d = jnp.where(slots[i] < count, d, 0.0)
                out[slots[i], w] = d.T.astype(BF16)

    pl.when(count > 0)(lambda: sweep(of(va), end_three))
    c = pltpu.make_async_copy(out, out_hbm, out_sems.at[0])
    c.start()
    c.wait()


def shift(value, step):
    size = lax.axis_size("grp") * lax.axis_size("sub")
    return lax.ppermute(value, AXES, [(s, (s + step) % size) for s in range(size)])


def mate_of(value):
    return lax.ppermute(value, "sub", [(s, s ^ 1) for s in range(lax.axis_size("sub"))])


def body(ham_columns, bond_mask, owned_counts, fermi_level):
    smem = pl.BlockSpec(memory_space=pltpu.SMEM)
    vmem = pl.BlockSpec(memory_space=pltpu.VMEM)
    hbm = pl.BlockSpec(memory_space=pltpu.HBM)
    on_chip = lambda *a: [pltpu.with_memory_space_constraint(v, pltpu.VMEM) for v in a]
    mate_bond = mate_of(bond_mask)
    mate_ham = mate_of(ham_columns)
    up, down, local, bits = pl.pallas_call(
        pack_kernel,
        out_shape=(
            pltpu.VMEM((1296, 128), BF16),
            pltpu.VMEM((640, 128), BF16),
            pltpu.VMEM((20, 128, 128), BF16),
            pltpu.VMEM((16, 128), F32),
        ),
        in_specs=[smem, vmem, vmem, vmem, vmem],
        out_specs=(vmem,) * 4,
        name="pack",
    )(owned_counts, bond_mask, *on_chip(mate_bond), ham_columns, *on_chip(mate_ham))
    up_got = shift(up, 2)
    down_got = shift(down, -2)
    up_got, down_got = lax.optimization_barrier((up_got, down_got))
    mate_up = mate_of(up_got)
    mate_down = mate_of(down_got)
    return pl.pallas_call(
        main_kernel,
        out_shape=jax.ShapeDtypeStruct((3, 9, 128, 128), BF16),
        in_specs=[smem, smem] + [vmem] * 6,
        out_specs=hbm,
        scratch_shapes=[
            pltpu.VMEM((32, 128), F32),
            pltpu.VMEM((1664, 1664), BF16),
            pltpu.VMEM((384, 1536), F32),
            pltpu.VMEM((384, 1536), F32),
            pltpu.VMEM((384, 1536), BF16),
            pltpu.VMEM((384, 1536), BF16),
            pltpu.VMEM((8, 1536), F32),
            pltpu.VMEM((3, 9, 128, 128), BF16),
            pltpu.SemaphoreType.DMA((1,)),
        ],
        name="columns",
    )(owned_counts, fermi_level, *on_chip(local, bits, up_got, mate_up, down_got, mate_down))


def solution(mesh):
    placed = (P(AXES, None, None, None), P(AXES, None), P(), P())
    return jax.shard_map(
        body,
        mesh=mesh,
        in_specs=placed,
        out_specs=P(AXES, None, None, None),
        check_vma=False,
    )
```

time: 48.3 us -> 38 us (0.79)
  waiting for transfers between devices: 21.8 us -> 8.9 us
  starting transfers between devices: 6.47 us -> 12.8 us
  local copies, waits for them, and re-layouts: 4.12 us -> 1.36 us
  Pallas kernels: 14.9 us -> 13.9 us
    ppermute x2, waiting for transfers between devices: 21 us -> 7.72 us  [shift(): lax.ppermute(value, AXES, [(s, (s + step) % size) for s in range(size)])]
    ppermute x2, starting transfers between devices: 1.47 us -> 8.67 us  [shift(): lax.ppermute(value, AXES, [(s, (s + step) % size) for s in range(size)])]
    unnamed x13 -> x1, local copies, waits for them, and re-layouts: 4.12 us -> 1.36 us
    ppermute x4, starting transfers between devices: 5.01 us -> 4.15 us  [mate_of(): lax.ppermute(value, 'sub', [(s, s ^ 1) for s in range(lax.axis_size('sub'...]
    pallas_call x1, Pallas kernels: 2.15 us -> 1.33 us  [body(): pl.pallas_call(pack_kernel, out_shape=(pltpu.VMEM((1296, 128), BF16), plt...]
  transfers between devices with their start and end apart: 6 -> 6, of which waited for: 4 -> 4; matrix products, arithmetic and copies ran while one was open for 3% -> 4% of each run, Pallas kernels for 0% -> 0%
where the time goes in v2:
time: 38 us; the launch traced here: 37.7 us
  Pallas kernels  13.9 us (37%)
  starting transfers between devices  12.8 us (34%)
  waiting for transfers between devices  8.9 us (23%)
  local copies, waits for them, and re-layouts  1.36 us (4%)
  between operations  0.67 us (2%)
    pallas_call x1, Pallas kernels, body(): pl.pallas_call(main_kernel, out_shape=jax.ShapeDtypeStruct((3, 9, 128, 12...  12.6 us
    ppermute x2, starting transfers between devices, shift(): lax.ppermute(value, AXES, [(s, (s + step) % size) for s in range(size)])  8.67 us
    ppermute x2, waiting for transfers between devices, shift(): lax.ppermute(value, AXES, [(s, (s + step) % size) for s in range(size)])  7.72 us
    ppermute x4, starting transfers between devices, mate_of(): lax.ppermute(value, 'sub', [(s, s ^ 1) for s in range(lax.axis_size('sub'...  4.15 us
    unnamed x1, local copies, waits for them, and re-layouts  1.36 us
    pallas_call x1, Pallas kernels, body(): pl.pallas_call(pack_kernel, out_shape=(pltpu.VMEM((1296, 128), BF16), plt...  1.33 us
    ppermute x4, waiting for transfers between devices, mate_of(): lax.ppermute(value, 'sub', [(s, s ^ 1) for s in range(lax.axis_size('sub'...  1.18 us
  transfers between devices with their start and end apart: 6, of which 4 were waited for; matrix products, arithmetic and copies ran while one was open for 4% of the time, Pallas kernels for 0%

profile of v2, /device:TPU:1, one launch (start us, length us, event | category | flops | bytes accessed | tf_op | source)
XLA Modules:
  0.0 37.7 jit_solution(6398297194504820294)
XLA Ops:
  0.0 3.2 %collective-permute-start.1 = (bf16[3,5,128,128]{3,2,1,0:T(8,128)(2,1)}, bf16[3,5,128,128]{3,2,1,0:T(8,128)(2,1)S(1)}, u32[]{:S(2)}, u32[]{:S(2)}) collective-permute-start(bf16[3,5,128,128]{3,2,1,0:T(8,128)(2,1)} %ham_ref.1), channel_id=1, source_target_pairs={{0,1},{1,0},{2,3},{3,2},{4,5},{5,4},{6,7},{7,6},{8,9},{9,8},{10,11... | collective-permute-start | bytes 1474568 | tf_op jit(solution)/shard_map/ppermute | solution.py:194
  3.2 0.0 collective-permute-start
  3.2 1.4 %copy.6.counts_ref = s32[32,8]{1,0:T(8,128)} copy(s32[32,8]{0,1:T(8,128)} %param.6) | data formatting | bytes 2048 | tf_op args[2]
  4.6 0.3 collective-permute-done.mate_bond_ref
  4.9 0.0 collective-permute-done.1.mate_ref
  4.9 1.3 %pack.1 = (bf16[1296,128]{1,0:T(8,128)(2,1)S(1)}, bf16[640,128]{1,0:T(8,128)(2,1)S(1)}, bf16[20,128,128]{2,1,0:T(8,128)(2,1)S(1)}, f32[16,128]{1,0:T(8,128)S(1)}) custom-call(s32[32,8]{1,0:T(8,128)} %copy.6.counts_ref, s32[3,4]{1,0:T(4,128)} %bond_ref.1, s32[3,4]{1,0:T(4,128)S(1)} %collective-permute-done.mate_bond_ref, bf16[3,5,128,128]{3,2,1,0:T(8,128)(2,1)} %ham_ref.1, ...), custom_call_target="tpu_custom_call" | custom-call | tf_op jit(solution)/shard_map/pack/pallas_call | solution.py:204
  6.2 0.1 collective-permute-start.2
  6.3 8.6 %collective-permute-start.3 = (bf16[640,128]{1,0:T(8,128)(2,1)S(1)}, bf16[640,128]{1,0:T(8,128)(2,1)S(1)}, u32[]{:S(2)}, u32[]{:S(2)}) collective-permute-start(bf16[640,128]{1,0:T(8,128)(2,1)S(1)} %get-tuple-element.14), channel_id=1, source_target_pairs={{0,254},{1,255},{2,0},{3,1},{4,2},{5,3},{6,4},{7,5},{8,6},{9,7},{1... | collective-permute-start | bytes 491528 | tf_op jit(solution)/shard_map/ppermute | solution.py:190
  14.9 3.2 %collective-permute-done.3.down_ref = bf16[640,128]{1,0:T(8,128)(2,1)S(1)} collective-permute-done((bf16[640,128]{1,0:T(8,128)(2,1)S(1)}, bf16[640,128]{1,0:T(8,128)(2,1)S(1)}, u32[]{:S(2)}, u32[]{:S(2)}) %collective-permute-start.3) | collective-permute-done | bytes 163872 | tf_op jit(solution)/shard_map/ppermute | solution.py:190
  18.1 4.5 %collective-permute-done.2.up_ref = bf16[1296,128]{1,0:T(8,128)(2,1)S(1)} collective-permute-done((bf16[1296,128]{1,0:T(8,128)(2,1)S(1)}, bf16[1296,128]{1,0:T(8,128)(2,1)S(1)}, u32[]{:S(2)}, u32[]{:S(2)}) %collective-permute-start.2) | collective-permute-done | bytes 331808 | tf_op jit(solution)/shard_map/ppermute | solution.py:190
  22.6 0.9 %collective-permute-start.4 = (bf16[1296,128]{1,0:T(8,128)(2,1)S(1)}, bf16[1296,128]{1,0:T(8,128)(2,1)S(1)}, u32[]{:S(2)}, u32[]{:S(2)}) collective-permute-start(bf16[1296,128]{1,0:T(8,128)(2,1)S(1)} %collective-permute-done.2.up_ref), channel_id=1, source_target_pairs={{0,1},{1,0},{2,3},{3,2},{4,5},{5,4},{6,7},{7,6},{8,9},{9,8},{10,11... | collective-permute-start | bytes 995336 | tf_op jit(solution)/shard_map/ppermute | solution.py:194
  23.6 0.0 collective-permute-start.5
  24.2 0.8 %collective-permute-done.5.mate_down_ref = bf16[640,128]{1,0:T(8,128)(2,1)S(1)} collective-permute-done((bf16[640,128]{1,0:T(8,128)(2,1)S(1)}, bf16[640,128]{1,0:T(8,128)(2,1)S(1)}, u32[]{:S(2)}, u32[]{:S(2)}) %collective-permute-start.5) | collective-permute-done | bytes 163872 | tf_op jit(solution)/shard_map/ppermute | solution.py:194
  25.1 0.0 collective-permute-done.4.mate_up_ref
  25.1 12.6 %columns.1 = bf16[3,9,128,128]{3,2,1,0:T(8,128)(2,1)} custom-call(s32[32,8]{1,0:T(8,128)} %copy.6.counts_ref, f32[1]{0:T(128)S(6)} %copy.7.mu_ref, bf16[20,128,128]{2,1,0:T(8,128)(2,1)S(1)} %get-tuple-element.11.local_ref, f32[16,128]{1,0:T(8,128)S(1)} %get-tuple-element.12.local_bits, bf16[1296,128]{1,0:T(8,128)(2,1)S(1)} %collective-permute-done.2.up_ref, ...), custom_call_target="tpu_custom_call" | custom-call | tf_op jit(solution)/shard_map/columns/pallas_call | solution.py:221
Async XLA Ops:
  0.0 4.9 %collective-permute-start.1 = (bf16[3,5,128,128]{3,2,1,0:T(8,128)(2,1)}, bf16[3,5,128,128]{3,2,1,0:T(8,128)(2,1)S(1)}, u32[]{:S(2)}, u32[]{:S(2)}) collective-permute-start(bf16[3,5,128,128]{3,2,1,0:T(8,128)(2,1)} %ham_ref.1), channel_id=1, source_target_pairs={{0,1},{1,0},{2,3},{3,2},{4,5},{5,4},{6,7},{7,6},{8,9},{9,8},{10,11... | collective-permute-start | bytes 1474568 | tf_op jit(solution)/shard_map/ppermute | solution.py:194
  3.2 1.7 %collective-permute-start = (s32[3,4]{1,0:T(4,128)}, s32[3,4]{1,0:T(4,128)S(1)}, u32[]{:S(2)}, u32[]{:S(2)}) collective-permute-start(s32[3,4]{1,0:T(4,128)} %bond_ref.1), channel_id=1, source_target_pairs={{0,1},{1,0},{2,3},{3,2},{4,5},{5,4},{6,7},{7,6},{8,9},{9,8},{10,11... | collective-permute-start | bytes 152 | tf_op jit(solution)/shard_map/ppermute | solution.py:194
  6.2 16.4 %collective-permute-start.2 = (bf16[1296,128]{1,0:T(8,128)(2,1)S(1)}, bf16[1296,128]{1,0:T(8,128)(2,1)S(1)}, u32[]{:S(2)}, u32[]{:S(2)}) collective-permute-start(bf16[1296,128]{1,0:T(8,128)(2,1)S(1)} %get-tuple-element.13), channel_id=1, source_target_pairs={{0,2},{1,3},{2,4},{3,5},{4,6},{5,7},{6,8},{7,9},{8,10},{9,11},{10,... | collective-permute-start | bytes 995336 | tf_op jit(solution)/shard_map/ppermute | solution.py:190
  6.3 11.8 %collective-permute-start.3 = (bf16[640,128]{1,0:T(8,128)(2,1)S(1)}, bf16[640,128]{1,0:T(8,128)(2,1)S(1)}, u32[]{:S(2)}, u32[]{:S(2)}) collective-permute-start(bf16[640,128]{1,0:T(8,128)(2,1)S(1)} %get-tuple-element.14), channel_id=1, source_target_pairs={{0,254},{1,255},{2,0},{3,1},{4,2},{5,3},{6,4},{7,5},{8,6},{9,7},{1... | collective-permute-start | bytes 491528 | tf_op jit(solution)/shard_map/ppermute | solution.py:190
  22.6 2.4 %collective-permute-start.4 = (bf16[1296,128]{1,0:T(8,128)(2,1)S(1)}, bf16[1296,128]{1,0:T(8,128)(2,1)S(1)}, u32[]{:S(2)}, u32[]{:S(2)}) collective-permute-start(bf16[1296,128]{1,0:T(8,128)(2,1)S(1)} %collective-permute-done.2.up_ref), channel_id=1, source_target_pairs={{0,1},{1,0},{2,3},{3,2},{4,5},{5,4},{6,7},{7,6},{8,9},{9,8},{10,11... | collective-permute-start | bytes 995336 | tf_op jit(solution)/shard_map/ppermute | solution.py:194
  23.6 1.5 %collective-permute-start.5 = (bf16[640,128]{1,0:T(8,128)(2,1)S(1)}, bf16[640,128]{1,0:T(8,128)(2,1)S(1)}, u32[]{:S(2)}, u32[]{:S(2)}) collective-permute-start(bf16[640,128]{1,0:T(8,128)(2,1)S(1)} %collective-permute-done.3.down_ref), channel_id=1, source_target_pairs={{0,1},{1,0},{2,3},{3,2},{4,5},{5,4},{6,7},{7,6},{8,9},{9,8},{10,11... | collective-permute-start | bytes 491528 | tf_op jit(solution)/shard_map/ppermute | solution.py:194

commit v3 on v2

v3 whole, which is shorter than its diff:
```python
import jax
import jax.numpy as jnp
from jax import lax
from jax.experimental import pallas as pl
from jax.experimental.pallas import tpu as pltpu
from jax.sharding import PartitionSpec as P


AXES = ("grp", "sub")
CHIP_COLS = 4
BF16 = jnp.bfloat16
F32 = jnp.float32

DOWN = (((0, 0), (0, 1), (1, 0), (0, 2), (0, 3)), ((1, 1), (1, 2), (2, 0), (2, 1), (3, 0)))


def place(counts_ref):
    group = lax.axis_index("grp")
    member = lax.axis_index("sub")
    parity = member % 2
    low = member - parity
    wraps = low == 0
    groups, members = counts_ref.shape
    before_group = jnp.where(wraps, jnp.where(group == 0, groups - 1, group - 1), group)
    before = counts_ref[before_group, jnp.where(wraps, members - 2, low - 2)]
    return parity, counts_ref[group, low], counts_ref[group, member], before


def rest_column(low_count, parity):
    return jnp.where(low_count == 1, 2, 1) + parity


def pack_kernel(counts_ref, bond_ref, mate_bond_ref, ham_ref, mate_ref, up_ref, down_ref, local_ref, bits_ref):
    parity, low_count, _, _ = place(counts_ref)
    for t in range(CHIP_COLS):
        in_low = t < low_count
        slot = jnp.where(in_low, t, t - low_count)
        mine = in_low == (parity == 0)
        bonds = jnp.where(mine, bond_ref[pl.ds(slot, 1), :], mate_bond_ref[pl.ds(slot, 1), :]).astype(F32)
        for o in range(5):
            value = jnp.where(mine, ham_ref[slot, o], mate_ref[slot, o])
            if o:
                row = jnp.broadcast_to(bonds[:, o - 1 : o], (1, 128))
                bits_ref[t * 4 + o - 1 : t * 4 + o, :] = row
                value = value * row.astype(BF16)
            local_ref[t * 5 + o] = value
    rest = rest_column(low_count, parity)
    for k in range(5):
        up_ref[k * 128 : (k + 1) * 128, :] = local_ref[rest * 5 + k]
    up_ref[640:656, :] = bits_ref[...].astype(BF16)
    for k in range(5):
        (t, o), (tt, oo) = DOWN[0][k], DOWN[1][k]
        down_ref[k * 128 : (k + 1) * 128, :] = local_ref[jnp.where(parity == 0, t * 5 + o, tt * 5 + oo)]


def main_kernel(
    counts_ref, mu_ref, local_ref, local_bits, one_ref, mate_one_ref, up_ref, mate_up_ref, down_ref, mate_down_ref,
    keep_ref, send_ref, bits, cols, x, first, kept, va, vb, mask,
):
    parity, _, count, before = place(counts_ref)
    even = parity == 0
    shift = parity * 2

    bits[0:16, :] = up_ref[640:656, :].astype(F32)
    bits[16:32, :] = local_bits[...]

    def lane(own, mate, which):
        return jnp.where(parity == which, own, mate)

    for which in range(2):
        p = jnp.where(before == 1, 1, 3) if which else 0
        for o in range(5):
            value = lane(one_ref[0, o], mate_one_ref[0, o], which)
            if o:
                value = value * bits[pl.ds(p * 4 + o - 1, 1), :].astype(BF16)
            cols[p, o] = value
        p = rest_column(before, which)
        for o in range(5):
            rows = slice(o * 128, (o + 1) * 128)
            cols[p, o] = lane(up_ref[rows, :], mate_up_ref[rows, :], which)
        for k, (t, o) in enumerate(DOWN[which]):
            rows = slice(k * 128, (k + 1) * 128)
            cols[8 + t, o] = lane(down_ref[rows, :], mate_down_ref[rows, :], which)
    for t in range(CHIP_COLS):
        for o in range(5):
            cols[4 + t, o] = local_ref[t * 5 + o]

    for i in range(2):
        c = 4 + i
        for u in range(10):
            if u == c:
                row = jnp.ones((1, 128), F32)
            elif c < u <= c + 4:
                row = bits[pl.ds((c + shift) * 4 + (u - c - 1), 1), :]
            elif c - 4 <= u < c:
                row = bits[pl.ds((u + shift) * 4 + (c - u - 1), 1), :]
            else:
                row = jnp.zeros((1, 128), F32)
            mask[i : i + 1, u * 128 : (u + 1) * 128] = row

    mu = mu_ref[0]
    eye = (
        lax.broadcasted_iota(jnp.int32, (128, 128), 0) == lax.broadcasted_iota(jnp.int32, (128, 128), 1)
    ).astype(F32)
    zero = jnp.zeros((128, 128), BF16)

    def cell(i, j):
        return (slice(i * 128, (i + 1) * 128), slice(j * 128, (j + 1) * 128))

    @pl.when(count > 0)
    def _():
        for u in range(10):
            for v in range(u - 4):
                x[cell(u, v)] = zero
                x[cell(v, u)] = zero
        for u in range(10):
            x[cell(u, u)] = ((cols[u + shift, 0].astype(F32) - mu * eye) * 0.25).astype(BF16)
            for o in range(1, 5):
                if u + o < 10:
                    b = cols[u + shift, o] * jnp.asarray(0.25, BF16)
                    x[cell(u + o, u)] = b
                    x[cell(u, u + o)] = b.T

    def sweep(src, off, use):
        for n in range(5):
            k0, k1 = max(0, n - 2), min(5, n + 3)
            acc = jnp.dot(
                src[off : off + 256, k0 * 256 : k1 * 256],
                x[k0 * 256 : k1 * 256, n * 256 : (n + 1) * 256],
                preferred_element_type=F32,
            )
            for i in range(2):
                m = mask[i : i + 1, n * 256 : (n + 1) * 256]
                use(i, n, acc[i * 128 : (i + 1) * 128, :] * m)

    def sl(i, n):
        return (slice(i * 128, (i + 1) * 128), slice(n * 256, (n + 1) * 256))

    def store(ref):
        def use(i, n, part):
            ref[sl(i, n)] = part.astype(BF16)

        return use

    def end_one(i, n, part):
        f = x[512 + i * 128 : 512 + (i + 1) * 128, n * 256 : (n + 1) * 256].astype(F32)
        s = 1.5 * f - 0.5 * part
        kept[sl(i, n)] = s
        vb[sl(i, n)] = s.astype(BF16)

    def keep_first(ref):
        def use(i, n, part):
            first[sl(i, n)] = part
            ref[sl(i, n)] = part.astype(BF16)

        return use

    def end_two(i, n, part):
        va[sl(i, n)] = (1.5 * first[sl(i, n)] - 0.5 * part).astype(BF16)

    def end_three(targets):
        def use(i, n, part):
            s3 = 1.5 * first[sl(i, n)] - 0.5 * part
            y = 1.5 * kept[sl(i, n)] - 0.5 * s3
            for h in range(2):
                w = 2 * n + h - i
                if 0 <= w < 9:
                    d = -0.5 * y[:, h * 128 : (h + 1) * 128]
                    if w == 4:
                        d = d + 0.5 * eye
                    targets[i][w] = d.astype(BF16).T

        return use

    pl.when(count > 0)(lambda: sweep(x, 512, store(va)))
    pl.when(count > 0)(lambda: sweep(va, 0, end_one))
    pl.when(count > 0)(lambda: sweep(vb, 0, keep_first(va)))
    pl.when(count > 0)(lambda: sweep(va, 0, store(vb)))
    pl.when(count > 0)(lambda: sweep(vb, 0, end_two))
    pl.when(count > 0)(lambda: sweep(va, 0, keep_first(vb)))
    pl.when(count > 0)(lambda: sweep(vb, 0, store(va)))
    pl.when(even)(lambda: sweep(va, 0, end_three((keep_ref, send_ref))))
    pl.when(jnp.logical_not(even))(lambda: sweep(va, 0, end_three((send_ref, keep_ref))))


def place_kernel(counts_ref, keep_ref, send_ref, got_ref, out_hbm, zeros, sems):
    parity, _, count, _ = place(counts_ref)
    three = count == 3
    own = pltpu.make_async_copy(keep_ref, out_hbm.at[jnp.where(three, parity * 2, 0)], sems.at[0])
    own.start()

    @pl.when(three)
    def _():
        a = pltpu.make_async_copy(send_ref, out_hbm.at[1], sems.at[1])
        b = pltpu.make_async_copy(got_ref, out_hbm.at[2 - parity * 2], sems.at[2])
        a.start()
        b.start()
        a.wait()
        b.wait()

    @pl.when(jnp.logical_not(three))
    def _():
        zeros[...] = jnp.zeros(zeros.shape, BF16)
        a = pltpu.make_async_copy(zeros, out_hbm.at[1], sems.at[1])
        b = pltpu.make_async_copy(zeros, out_hbm.at[2], sems.at[2])
        a.start()
        b.start()
        a.wait()
        b.wait()

    own.wait()


def shift(value, step):
    size = lax.axis_size("grp") * lax.axis_size("sub")
    return lax.ppermute(value, AXES, [(s, (s + step) % size) for s in range(size)])


def mate_of(value):
    return lax.ppermute(value, "sub", [(s, s ^ 1) for s in range(lax.axis_size("sub"))])


def body(ham_columns, bond_mask, owned_counts, fermi_level):
    smem = pl.BlockSpec(memory_space=pltpu.SMEM)
    vmem = pl.BlockSpec(memory_space=pltpu.VMEM)
    hbm = pl.BlockSpec(memory_space=pltpu.HBM)
    on_chip = lambda *a: [pltpu.with_memory_space_constraint(v, pltpu.VMEM) for v in a]
    mate_bond = mate_of(bond_mask)
    mate_ham = mate_of(ham_columns)
    one_got = shift(ham_columns[0:1], 2)
    up, down, local, bits = pl.pallas_call(
        pack_kernel,
        out_shape=(
            pltpu.VMEM((656, 128), BF16),
            pltpu.VMEM((640, 128), BF16),
            pltpu.VMEM((20, 128, 128), BF16),
            pltpu.VMEM((16, 128), F32),
        ),
        in_specs=[smem, vmem, vmem, vmem, vmem],
        out_specs=(vmem,) * 4,
        name="pack",
    )(owned_counts, bond_mask, *on_chip(mate_bond), ham_columns, *on_chip(mate_ham))
    up_got = shift(up, 2)
    down_got = shift(down, -2)
    up_got, down_got = lax.optimization_barrier((up_got, down_got))
    mate_one = mate_of(one_got)
    mate_up = mate_of(up_got)
    mate_down = mate_of(down_got)
    keep, send = pl.pallas_call(
        main_kernel,
        out_shape=(pltpu.VMEM((9, 128, 128), BF16),) * 2,
        in_specs=[smem, smem] + [vmem] * 8,
        out_specs=(vmem,) * 2,
        scratch_shapes=[
            pltpu.VMEM((32, 128), F32),
            pltpu.VMEM((12, 5, 128, 128), BF16),
            pltpu.VMEM((1280, 1280), BF16),
            pltpu.VMEM((256, 1280), F32),
            pltpu.VMEM((256, 1280), F32),
            pltpu.VMEM((256, 1280), BF16),
            pltpu.VMEM((256, 1280), BF16),
            pltpu.VMEM((8, 1280), F32),
        ],
        name="columns",
    )(
        owned_counts,
        fermi_level,
        *on_chip(local, bits, one_got, mate_one, up_got, mate_up, down_got, mate_down),
    )
    got = mate_of(send)
    return pl.pallas_call(
        place_kernel,
        out_shape=jax.ShapeDtypeStruct((3, 9, 128, 128), BF16),
        in_specs=[smem] + [vmem] * 3,
        out_specs=hbm,
        scratch_shapes=[pltpu.VMEM((9, 128, 128), BF16), pltpu.SemaphoreType.DMA((3,))],
        name="place",
    )(owned_counts, *on_chip(keep, send, got))


def solution(mesh):
    placed = (P(AXES, None, None, None), P(AXES, None), P(), P())
    return jax.shard_map(
        body,
        mesh=mesh,
        in_specs=placed,
        out_specs=P(AXES, None, None, None),
        check_vma=False,
    )
```

time: 38 us -> 40.4 us (1.063)
  Pallas kernels: 13.9 us -> 10.3 us
  waiting for transfers between devices: 8.9 us -> 12 us
  starting transfers between devices: 12.8 us -> 14.7 us
  local copies, waits for them, and re-layouts: 1.36 us -> 2.29 us
    pallas_call x2 -> x3, Pallas kernels: 13.9 us -> 10.3 us  [the longest x1 7.1 us: body(): pl.pallas_call(main_kernel, out_shape=(pltpu.VMEM((9, 128, 128), BF16),)...]
    ppermute x2 -> x3, waiting for transfers between devices: 7.72 us -> 9.57 us  [shift(): lax.ppermute(value, AXES, [(s, (s + step) % size) for s in range(size)])]
    ppermute x4 -> x6, starting transfers between devices: 4.15 us -> 5.99 us  [mate_of(): lax.ppermute(value, 'sub', [(s, s ^ 1) for s in range(lax.axis_size('sub'...]
    ppermute x4 -> x6, waiting for transfers between devices: 1.18 us -> 2.42 us  [mate_of(): lax.ppermute(value, 'sub', [(s, s ^ 1) for s in range(lax.axis_size('sub'...]
    slice x0 -> x1, local copies, waits for them, and re-layouts: none -> 0.93 us  [body(): one_got = shift(ham_columns[0:1], 2)]
    ppermute x2 -> x3, starting transfers between devices: 8.67 us -> 8.76 us  [shift(): lax.ppermute(value, AXES, [(s, (s + step) % size) for s in range(size)])]
  transfers between devices with their start and end apart: 6 -> 9, of which waited for: 4 -> 7; matrix products, arithmetic and copies ran while one was open for 4% -> 6% of each run, Pallas kernels for 0% -> 0%
where the time goes in v3:
time: 40.4 us; the launch traced here: 40 us
  starting transfers between devices  14.7 us (36%)
  waiting for transfers between devices  12 us (30%)
  Pallas kernels  10.3 us (25%)
  local copies, waits for them, and re-layouts  2.29 us (6%)
  between operations  0.69 us (2%)
    ppermute x3, waiting for transfers between devices, shift(): lax.ppermute(value, AXES, [(s, (s + step) % size) for s in range(size)])  9.57 us
    ppermute x3, starting transfers between devices, shift(): lax.ppermute(value, AXES, [(s, (s + step) % size) for s in range(size)])  8.76 us
    pallas_call x1, Pallas kernels, body(): pl.pallas_call(main_kernel, out_shape=(pltpu.VMEM((9, 128, 128), BF16),)...  7.1 us
    ppermute x6, starting transfers between devices, mate_of(): lax.ppermute(value, 'sub', [(s, s ^ 1) for s in range(lax.axis_size('sub'...  5.99 us
    ppermute x6, waiting for transfers between devices, mate_of(): lax.ppermute(value, 'sub', [(s, s ^ 1) for s in range(lax.axis_size('sub'...  2.42 us
    pallas_call x1, Pallas kernels, body(): pl.pallas_call(place_kernel, out_shape=jax.ShapeDtypeStruct((3, 9, 128, 1...  1.88 us
    unnamed x1, local copies, waits for them, and re-layouts  1.37 us
    pallas_call x1, Pallas kernels, body(): pl.pallas_call(pack_kernel, out_shape=(pltpu.VMEM((656, 128), BF16), pltp...  1.3 us
  transfers between devices with their start and end apart: 9, of which 7 were waited for; matrix products, arithmetic and copies ran while one was open for 6% of the time, Pallas kernels for 0%

profile of v3, /device:TPU:1, one launch (start us, length us, event | category | flops | bytes accessed | tf_op | source)
XLA Modules:
  0.0 40.0 jit_solution(5365036435795549196)
XLA Ops:
  0.0 3.2 %collective-permute-start.1 = (bf16[3,5,128,128]{3,2,1,0:T(8,128)(2,1)}, bf16[3,5,128,128]{3,2,1,0:T(8,128)(2,1)S(1)}, u32[]{:S(2)}, u32[]{:S(2)}) collective-permute-start(bf16[3,5,128,128]{3,2,1,0:T(8,128)(2,1)} %ham_ref.1), channel_id=1, source_target_pairs={{0,1},{1,0},{2,3},{3,2},{4,5},{5,4},{6,7},{7,6},{8,9},{9,8},{10,11... | collective-permute-start | bytes 1474568 | tf_op jit(solution)/shard_map/ppermute | solution.py:220
  3.2 0.0 collective-permute-start
  3.2 1.4 %copy.7.counts_ref = s32[32,8]{1,0:T(8,128)} copy(s32[32,8]{0,1:T(8,128)} %param.6) | data formatting | bytes 2048 | tf_op args[2]
  4.6 0.3 collective-permute-done.mate_bond_ref
  4.9 0.0 collective-permute-done.1.mate_ref
  4.9 1.3 %pack.1 = (bf16[656,128]{1,0:T(8,128)(2,1)S(1)}, bf16[640,128]{1,0:T(8,128)(2,1)S(1)}, bf16[20,128,128]{2,1,0:T(8,128)(2,1)S(1)}, f32[16,128]{1,0:T(8,128)S(1)}) custom-call(s32[32,8]{1,0:T(8,128)} %copy.7.counts_ref, s32[3,4]{1,0:T(4,128)} %bond_ref.1, s32[3,4]{1,0:T(4,128)S(1)} %collective-permute-done.mate_bond_ref, bf16[3,5,128,128]{3,2,1,0:T(8,128)(2,1)} %ham_ref.1, ...), custom_call_target="tpu_custom_call" | custom-call | tf_op jit(solution)/shard_map/pack/pallas_call | solution.py:231
  6.2 0.1 collective-permute-start.4
  6.3 8.6 %collective-permute-start.5 = (bf16[640,128]{1,0:T(8,128)(2,1)S(1)}, bf16[640,128]{1,0:T(8,128)(2,1)S(1)}, u32[]{:S(2)}, u32[]{:S(2)}) collective-permute-start(bf16[640,128]{1,0:T(8,128)(2,1)S(1)} %get-tuple-element.16), channel_id=1, source_target_pairs={{0,254},{1,255},{2,0},{3,1},{4,2},{5,3},{6,4},{7,5},{8,6},{9,7},{1... | collective-permute-start | bytes 491528 | tf_op jit(solution)/shard_map/ppermute | solution.py:216
  14.9 0.9 %slice.3 = bf16[1,5,128,128]{3,2,1,0:T(8,128)(2,1)S(1)} slice(bf16[3,5,128,128]{3,2,1,0:T(8,128)(2,1)} %ham_ref.1), slice={[0:1], [0:5], [0:128], [0:128]} | slice | bytes 327680 | tf_op jit(solution)/shard_map/slice | solution.py:230
  15.8 0.1 collective-permute-start.2
  15.9 2.2 %collective-permute-done.5.down_ref = bf16[640,128]{1,0:T(8,128)(2,1)S(1)} collective-permute-done((bf16[640,128]{1,0:T(8,128)(2,1)S(1)}, bf16[640,128]{1,0:T(8,128)(2,1)S(1)}, u32[]{:S(2)}, u32[]{:S(2)}) %collective-permute-start.5) | collective-permute-done | bytes 163872 | tf_op jit(solution)/shard_map/ppermute | solution.py:216
  18.1 1.0 %collective-permute-done.4.up_ref = bf16[656,128]{1,0:T(8,128)(2,1)S(1)} collective-permute-done((bf16[656,128]{1,0:T(8,128)(2,1)S(1)}, bf16[656,128]{1,0:T(8,128)(2,1)S(1)}, u32[]{:S(2)}, u32[]{:S(2)}) %collective-permute-start.4) | collective-permute-done | bytes 167968 | tf_op jit(solution)/shard_map/ppermute | solution.py:216
  19.1 0.9 %collective-permute-start.6 = (bf16[656,128]{1,0:T(8,128)(2,1)S(1)}, bf16[656,128]{1,0:T(8,128)(2,1)S(1)}, u32[]{:S(2)}, u32[]{:S(2)}) collective-permute-start(bf16[656,128]{1,0:T(8,128)(2,1)S(1)} %collective-permute-done.4.up_ref), channel_id=1, source_target_pairs={{0,1},{1,0},{2,3},{3,2},{4,5},{5,4},{6,7},{7,6},{8,9},{9,8},{10,11... | collective-permute-start | bytes 503816 | tf_op jit(solution)/shard_map/ppermute | solution.py:220
  20.0 6.4 %collective-permute-done.2.one_ref = bf16[1,5,128,128]{3,2,1,0:T(8,128)(2,1)S(1)} collective-permute-done((bf16[1,5,128,128]{3,2,1,0:T(8,128)(2,1)S(1)}, bf16[1,5,128,128]{3,2,1,0:T(8,128)(2,1)S(1)}, u32[]{:S(2)}, u32[]{:S(2)}) %collective-permute-start.2) | collective-permute-done | bytes 163872 | tf_op jit(solution)/shard_map/ppermute | solution.py:216
  26.4 1.5 %collective-permute-start.3 = (bf16[1,5,128,128]{3,2,1,0:T(8,128)(2,1)S(1)}, bf16[1,5,128,128]{3,2,1,0:T(8,128)(2,1)S(1)}, u32[]{:S(2)}, u32[]{:S(2)}) collective-permute-start(bf16[1,5,128,128]{3,2,1,0:T(8,128)(2,1)S(1)} %collective-permute-done.2.one_ref), channel_id=1, source_target_pairs={{0,1},{1,0},{2,3},{3,2},{4,5},{5,4},{6,7},{7,6},{8,9},{9,8},{10,11... | collective-permute-start | bytes 491528 | tf_op jit(solution)/shard_map/ppermute | solution.py:220
  27.9 0.0 collective-permute-start.7
  28.6 0.4 collective-permute-done.3.mate_one_ref
  29.0 0.4 collective-permute-done.7.mate_down_ref
  29.3 0.0 collective-permute-done.6.mate_up_ref
  29.3 7.1 %columns.1 = (bf16[9,128,128]{2,1,0:T(8,128)(2,1)S(1)}, bf16[9,128,128]{2,1,0:T(8,128)(2,1)S(1)}) custom-call(s32[32,8]{1,0:T(8,128)} %copy.7.counts_ref, f32[1]{0:T(128)S(6)} %copy.8.mu_ref, bf16[20,128,128]{2,1,0:T(8,128)(2,1)S(1)} %get-tuple-element.13.local_ref, f32[16,128]{1,0:T(8,128)S(1)} %get-tuple-element.14.local_bits, ...), custom_call_target="tpu_custom_call" | custom-call | tf_op jit(solution)/shard_map/columns/pallas_call | solution.py:249
  36.4 0.3 collective-permute-start.8
  36.8 1.3 %collective-permute-done.8.got_ref = bf16[9,128,128]{2,1,0:T(8,128)(2,1)S(1)} collective-permute-done((bf16[9,128,128]{2,1,0:T(8,128)(2,1)S(1)}, bf16[9,128,128]{2,1,0:T(8,128)(2,1)S(1)}, u32[]{:S(2)}, u32[]{:S(2)}) %collective-permute-start.8) | collective-permute-done | bytes 294944 | tf_op jit(solution)/shard_map/ppermute | solution.py:220
  38.1 1.9 %place.1 = bf16[3,9,128,128]{3,2,1,0:T(8,128)(2,1)} custom-call(s32[32,8]{1,0:T(8,128)} %copy.7.counts_ref, bf16[9,128,128]{2,1,0:T(8,128)(2,1)S(1)} %get-tuple-element.19.keep_ref, bf16[9,128,128]{2,1,0:T(8,128)(2,1)S(1)} %get-tuple-element.20.send_ref, bf16[9,128,128]{2,1,0:T(8,128)(2,1)S(1)} %collective-permute-done.8.got_ref), custom_call_target="tpu_custom_call" | custom-call | tf_op jit(solution)/shard_map/place/pallas_call | solution.py:271
Async XLA Ops:
  0.0 4.9 %collective-permute-start.1 = (bf16[3,5,128,128]{3,2,1,0:T(8,128)(2,1)}, bf16[3,5,128,128]{3,2,1,0:T(8,128)(2,1)S(1)}, u32[]{:S(2)}, u32[]{:S(2)}) collective-permute-start(bf16[3,5,128,128]{3,2,1,0:T(8,128)(2,1)} %ham_ref.1), channel_id=1, source_target_pairs={{0,1},{1,0},{2,3},{3,2},{4,5},{5,4},{6,7},{7,6},{8,9},{9,8},{10,11... | collective-permute-start | bytes 1474568 | tf_op jit(solution)/shard_map/ppermute | solution.py:220
  3.2 1.7 %collective-permute-start = (s32[3,4]{1,0:T(4,128)}, s32[3,4]{1,0:T(4,128)S(1)}, u32[]{:S(2)}, u32[]{:S(2)}) collective-permute-start(s32[3,4]{1,0:T(4,128)} %bond_ref.1), channel_id=1, source_target_pairs={{0,1},{1,0},{2,3},{3,2},{4,5},{5,4},{6,7},{7,6},{8,9},{9,8},{10,11... | collective-permute-start | bytes 152 | tf_op jit(solution)/shard_map/ppermute | solution.py:220
  6.2 12.9 %collective-permute-start.4 = (bf16[656,128]{1,0:T(8,128)(2,1)S(1)}, bf16[656,128]{1,0:T(8,128)(2,1)S(1)}, u32[]{:S(2)}, u32[]{:S(2)}) collective-permute-start(bf16[656,128]{1,0:T(8,128)(2,1)S(1)} %get-tuple-element.15), channel_id=1, source_target_pairs={{0,2},{1,3},{2,4},{3,5},{4,6},{5,7},{6,8},{7,9},{8,10},{9,11},{10,... | collective-permute-start | bytes 503816 | tf_op jit(solution)/shard_map/ppermute | solution.py:216
  6.3 11.8 %collective-permute-start.5 = (bf16[640,128]{1,0:T(8,128)(2,1)S(1)}, bf16[640,128]{1,0:T(8,128)(2,1)S(1)}, u32[]{:S(2)}, u32[]{:S(2)}) collective-permute-start(bf16[640,128]{1,0:T(8,128)(2,1)S(1)} %get-tuple-element.16), channel_id=1, source_target_pairs={{0,254},{1,255},{2,0},{3,1},{4,2},{5,3},{6,4},{7,5},{8,6},{9,7},{1... | collective-permute-start | bytes 491528 | tf_op jit(solution)/shard_map/ppermute | solution.py:216
  15.8 10.6 %collective-permute-start.2 = (bf16[1,5,128,128]{3,2,1,0:T(8,128)(2,1)S(1)}, bf16[1,5,128,128]{3,2,1,0:T(8,128)(2,1)S(1)}, u32[]{:S(2)}, u32[]{:S(2)}) collective-permute-start(bf16[1,5,128,128]{3,2,1,0:T(8,128)(2,1)S(1)} %slice.3), channel_id=1, source_target_pairs={{0,2},{1,3},{2,4},{3,5},{4,6},{5,7},{6,8},{7,9},{8,10},{9,11},{10,... | collective-permute-start | bytes 491528 | tf_op jit(solution)/shard_map/ppermute | solution.py:216
  19.1 10.2 %collective-permute-start.6 = (bf16[656,128]{1,0:T(8,128)(2,1)S(1)}, bf16[656,128]{1,0:T(8,128)(2,1)S(1)}, u32[]{:S(2)}, u32[]{:S(2)}) collective-permute-start(bf16[656,128]{1,0:T(8,128)(2,1)S(1)} %collective-permute-done.4.up_ref), channel_id=1, source_target_pairs={{0,1},{1,0},{2,3},{3,2},{4,5},{5,4},{6,7},{7,6},{8,9},{9,8},{10,11... | collective-permute-start | bytes 503816 | tf_op jit(solution)/shard_map/ppermute | solution.py:220
  26.4 2.5 %collective-permute-start.3 = (bf16[1,5,128,128]{3,2,1,0:T(8,128)(2,1)S(1)}, bf16[1,5,128,128]{3,2,1,0:T(8,128)(2,1)S(1)}, u32[]{:S(2)}, u32[]{:S(2)}) collective-permute-start(bf16[1,5,128,128]{3,2,1,0:T(8,128)(2,1)S(1)} %collective-permute-done.2.one_ref), channel_id=1, source_target_pairs={{0,1},{1,0},{2,3},{3,2},{4,5},{5,4},{6,7},{7,6},{8,9},{9,8},{10,11... | collective-permute-start | bytes 491528 | tf_op jit(solution)/shard_map/ppermute | solution.py:220
  27.9 1.4 %collective-permute-start.7 = (bf16[640,128]{1,0:T(8,128)(2,1)S(1)}, bf16[640,128]{1,0:T(8,128)(2,1)S(1)}, u32[]{:S(2)}, u32[]{:S(2)}) collective-permute-start(bf16[640,128]{1,0:T(8,128)(2,1)S(1)} %collective-permute-done.5.down_ref), channel_id=1, source_target_pairs={{0,1},{1,0},{2,3},{3,2},{4,5},{5,4},{6,7},{7,6},{8,9},{9,8},{10,11... | collective-permute-start | bytes 491528 | tf_op jit(solution)/shard_map/ppermute | solution.py:220
  36.4 1.7 %collective-permute-start.8 = (bf16[9,128,128]{2,1,0:T(8,128)(2,1)S(1)}, bf16[9,128,128]{2,1,0:T(8,128)(2,1)S(1)}, u32[]{:S(2)}, u32[]{:S(2)}) collective-permute-start(bf16[9,128,128]{2,1,0:T(8,128)(2,1)S(1)} %get-tuple-element.20.send_ref), channel_id=1, source_target_pairs={{0,1},{1,0},{2,3},{3,2},{4,5},{5,4},{6,7},{7,6},{8,9},{9,8},{10,11... | collective-permute-start | bytes 884744 | tf_op jit(solution)/shard_map/ppermute | solution.py:220

commit v4 on v3

--- a/solution.py
+++ b/solution.py
@@ -172,18 +172,21 @@
 
         return use
 
-    pl.when(count > 0)(lambda: sweep(x, 512, store(va)))
-    pl.when(count > 0)(lambda: sweep(va, 0, end_one))
-    pl.when(count > 0)(lambda: sweep(vb, 0, keep_first(va)))
-    pl.when(count > 0)(lambda: sweep(va, 0, store(vb)))
-    pl.when(count > 0)(lambda: sweep(vb, 0, end_two))
-    pl.when(count > 0)(lambda: sweep(va, 0, keep_first(vb)))
-    pl.when(count > 0)(lambda: sweep(vb, 0, store(va)))
+    @pl.when(count > 0)
+    def _():
+        sweep(x, 512, store(va))
+        sweep(va, 0, end_one)
+        sweep(vb, 0, keep_first(va))
+        sweep(va, 0, store(vb))
+        sweep(vb, 0, end_two)
+        sweep(va, 0, keep_first(vb))
+        sweep(vb, 0, store(va))
+
     pl.when(even)(lambda: sweep(va, 0, end_three((keep_ref, send_ref))))
     pl.when(jnp.logical_not(even))(lambda: sweep(va, 0, end_three((send_ref, keep_ref))))
 
 
-def place_kernel(counts_ref, keep_ref, send_ref, got_ref, out_hbm, zeros, sems):
+def put_kernel(counts_ref, keep_ref, send_ref, out_hbm, zeros, sems):
     parity, _, count, _ = place(counts_ref)
     three = count == 3
     own = pltpu.make_async_copy(keep_ref, out_hbm.at[jnp.where(three, parity * 2, 0)], sems.at[0])
@@ -192,21 +195,15 @@
     @pl.when(three)
     def _():
         a = pltpu.make_async_copy(send_ref, out_hbm.at[1], sems.at[1])
-        b = pltpu.make_async_copy(got_ref, out_hbm.at[2 - parity * 2], sems.at[2])
         a.start()
-        b.start()
         a.wait()
-        b.wait()
 
     @pl.when(jnp.logical_not(three))
     def _():
         zeros[...] = jnp.zeros(zeros.shape, BF16)
         a = pltpu.make_async_copy(zeros, out_hbm.at[1], sems.at[1])
-        b = pltpu.make_async_copy(zeros, out_hbm.at[2], sems.at[2])
         a.start()
-        b.start()
         a.wait()
-        b.wait()
 
     own.wait()
 
@@ -242,10 +239,13 @@
     )(owned_counts, bond_mask, *on_chip(mate_bond), ham_columns, *on_chip(mate_ham))
     up_got = shift(up, 2)
     down_got = shift(down, -2)
-    up_got, down_got = lax.optimization_barrier((up_got, down_got))
     mate_one = mate_of(one_got)
+    mate_down = mate_of(down_got)
+    parity, _, count, _ = place(owned_counts)
+    three = count == 3
+    slot = jnp.where(jnp.logical_and(three, parity == 1), 0, 2)
+    up_got, mate_one, mate_down, three, slot = lax.optimization_barrier((up_got, mate_one, mate_down, three, slot))
     mate_up = mate_of(up_got)
-    mate_down = mate_of(down_got)
     keep, send = pl.pallas_call(
         main_kernel,
         out_shape=(pltpu.VMEM((9, 128, 128), BF16),) * 2,
@@ -268,14 +268,17 @@
         *on_chip(local, bits, one_got, mate_one, up_got, mate_up, down_got, mate_down),
     )
     got = mate_of(send)
-    return pl.pallas_call(
-        place_kernel,
-        out_shape=jax.ShapeDtypeStruct((3, 9, 128, 128), BF16),
-        in_specs=[smem] + [vmem] * 3,
+    shape = jax.ShapeDtypeStruct((3, 9, 128, 128), BF16)
+    partial = pl.pallas_call(
+        put_kernel,
+        out_shape=shape,
+        in_specs=[smem, vmem, vmem],
         out_specs=hbm,
         scratch_shapes=[pltpu.VMEM((9, 128, 128), BF16), pltpu.SemaphoreType.DMA((3,))],
-        name="place",
-    )(owned_counts, *on_chip(keep, send, got))
+        name="put",
+    )(owned_counts, *on_chip(keep, send))
+    last = jnp.where(three, got, jnp.zeros_like(got))
+    return lax.dynamic_update_slice(partial, last[None], (slot, 0, 0, 0))
 
 
 def solution(mesh):

time: 40.4 us -> 38.6 us (0.955)
  waiting for transfers between devices: 12 us -> 7.42 us
  starting transfers between devices: 14.7 us -> 16.3 us
  other arithmetic: 0 us -> 0.78 us
  between operations: 0.69 us -> 1.38 us
    ppermute x3, waiting for transfers between devices: 9.57 us -> 7.02 us  [shift(): lax.ppermute(value, AXES, [(s, (s + step) % size) for s in range(size)])]
    ppermute x6, waiting for transfers between devices: 2.42 us -> 0.4 us  [mate_of(): lax.ppermute(value, 'sub', [(s, s ^ 1) for s in range(lax.axis_size('sub'...]
    ppermute x6, starting transfers between devices: 5.99 us -> 7.52 us  [mate_of(): lax.ppermute(value, 'sub', [(s, s ^ 1) for s in range(lax.axis_size('sub'...]
    dynamic_update_slice x0 -> x1, other arithmetic: none -> 0.78 us  [body(): return lax.dynamic_update_slice(partial, last[None], (slot, 0, 0, 0))]
    unnamed x1 -> x3, local copies, waits for them, and re-layouts: 1.37 us -> 0.68 us
    dynamic_slice x0 -> x1, local copies, waits for them, and re-layouts: none -> 0.58 us  [place(): return (parity, counts_ref[group, low], counts_ref[group, member], before)]
  transfers between devices with their start and end apart: 9 -> 9, of which waited for: 7 -> 4; matrix products, arithmetic and copies ran while one was open for 6% -> 6% of each run, Pallas kernels for 0% -> 8%
where the time goes in v4:
time: 38.6 us; the launch traced here: 38.2 us
  starting transfers between devices  16.3 us (42%)
  Pallas kernels  10.2 us (26%)
  waiting for transfers between devices  7.42 us (19%)
  local copies, waits for them, and re-layouts  2.19 us (6%)
  between operations  1.38 us (4%)
  other arithmetic  0.78 us (2%)
    ppermute x3, starting transfers between devices, shift(): lax.ppermute(value, AXES, [(s, (s + step) % size) for s in range(size)])  8.76 us
    ppermute x6, starting transfers between devices, mate_of(): lax.ppermute(value, 'sub', [(s, s ^ 1) for s in range(lax.axis_size('sub'...  7.52 us
    pallas_call x1, Pallas kernels, body(): pl.pallas_call(main_kernel, out_shape=(pltpu.VMEM((9, 128, 128), BF16),)...  7.08 us
    ppermute x3, waiting for transfers between devices, shift(): lax.ppermute(value, AXES, [(s, (s + step) % size) for s in range(size)])  7.02 us
    pallas_call x1, Pallas kernels, body(): pl.pallas_call(put_kernel, out_shape=shape, in_specs=[smem, vmem, vmem],...  1.78 us
    pallas_call x1, Pallas kernels, body(): pl.pallas_call(pack_kernel, out_shape=(pltpu.VMEM((656, 128), BF16), pltp...  1.3 us
    slice x1, local copies, waits for them, and re-layouts, body(): one_got = shift(ham_columns[0:1], 2)  0.93 us
    dynamic_update_slice x1, other arithmetic, body(): return lax.dynamic_update_slice(partial, last[None], (slot, 0, 0, 0))  0.78 us
  transfers between devices with their start and end apart: 9, of which 4 were waited for; matrix products, arithmetic and copies ran while one was open for 6% of the time, Pallas kernels for 8%

profile of v4, /device:TPU:1, one launch (start us, length us, event | category | flops | bytes accessed | tf_op | source)
XLA Modules:
  0.0 38.2 jit_solution(13961868813660335531)
XLA Ops:
  0.0 0.0 copy-start
  0.0 3.2 %collective-permute-start.1 = (bf16[3,5,128,128]{3,2,1,0:T(8,128)(2,1)}, bf16[3,5,128,128]{3,2,1,0:T(8,128)(2,1)S(1)}, u32[]{:S(2)}, u32[]{:S(2)}) collective-permute-start(bf16[3,5,128,128]{3,2,1,0:T(8,128)(2,1)} %ham_ref.1), channel_id=1, source_target_pairs={{0,1},{1,0},{2,3},{3,2},{4,5},{5,4},{6,7},{7,6},{8,9},{9,8},{10,11... | collective-permute-start | bytes 1474568 | tf_op jit(solution)/shard_map/ppermute | solution.py:217
  3.2 0.0 collective-permute-start
  3.2 0.9 %slice.3 = bf16[1,5,128,128]{3,2,1,0:T(8,128)(2,1)S(1)} slice(bf16[3,5,128,128]{3,2,1,0:T(8,128)(2,1)} %ham_ref.1), slice={[0:1], [0:5], [0:128], [0:128]} | slice | bytes 327680 | tf_op jit(solution)/shard_map/slice | solution.py:227
  4.1 0.1 collective-permute-start.2
  4.2 0.0 copy-done
  4.2 0.7 %copy.7.counts_ref = s32[32,8]{1,0:T(8,128)} copy(s32[32,8]{0,1:T(8,128)S(1)} %copy-done) | data formatting | bytes 2048 | tf_op args[2]
  4.9 0.0 collective-permute-done.mate_bond_ref
  4.9 0.0 collective-permute-done.1.mate_ref
  4.9 1.3 %pack.1 = (bf16[656,128]{1,0:T(8,128)(2,1)S(1)}, bf16[640,128]{1,0:T(8,128)(2,1)S(1)}, bf16[20,128,128]{2,1,0:T(8,128)(2,1)S(1)}, f32[16,128]{1,0:T(8,128)S(1)}) custom-call(s32[32,8]{1,0:T(8,128)} %copy.7.counts_ref, s32[3,4]{1,0:T(4,128)} %bond_ref.1, s32[3,4]{1,0:T(4,128)S(1)} %collective-permute-done.mate_bond_ref, bf16[3,5,128,128]{3,2,1,0:T(8,128)(2,1)} %ham_ref.1, ...), custom_call_target="tpu_custom_call" | custom-call | tf_op jit(solution)/shard_map/pack/pallas_call | solution.py:228
  6.2 8.7 %collective-permute-start.5 = (bf16[640,128]{1,0:T(8,128)(2,1)S(1)}, bf16[640,128]{1,0:T(8,128)(2,1)S(1)}, u32[]{:S(2)}, u32[]{:S(2)}) collective-permute-start(bf16[640,128]{1,0:T(8,128)(2,1)S(1)} %get-tuple-element.19), channel_id=1, source_target_pairs={{0,254},{1,255},{2,0},{3,1},{4,2},{5,3},{6,4},{7,5},{8,6},{9,7},{1... | collective-permute-start | bytes 491528 | tf_op jit(solution)/shard_map/ppermute | solution.py:213
  14.9 0.0 collective-permute-start.3
  14.9 2.1 %collective-permute-done.2.one_ref = bf16[1,5,128,128]{3,2,1,0:T(8,128)(2,1)S(1)} collective-permute-done((bf16[1,5,128,128]{3,2,1,0:T(8,128)(2,1)S(1)}, bf16[1,5,128,128]{3,2,1,0:T(8,128)(2,1)S(1)}, u32[]{:S(2)}, u32[]{:S(2)}) %collective-permute-start.2) | collective-permute-done | bytes 163872 | tf_op jit(solution)/shard_map/ppermute | solution.py:213
  17.0 1.0 %collective-permute-start.4 = (bf16[1,5,128,128]{3,2,1,0:T(8,128)(2,1)S(1)}, bf16[1,5,128,128]{3,2,1,0:T(8,128)(2,1)S(1)}, u32[]{:S(2)}, u32[]{:S(2)}) collective-permute-start(bf16[1,5,128,128]{3,2,1,0:T(8,128)(2,1)S(1)} %collective-permute-done.2.one_ref), channel_id=1, source_target_pairs={{0,1},{1,0},{2,3},{3,2},{4,5},{5,4},{6,7},{7,6},{8,9},{9,8},{10,11... | collective-permute-start | bytes 491528 | tf_op jit(solution)/shard_map/ppermute | solution.py:217
  18.0 0.1 collective-permute-done.5.down_ref
  18.0 1.3 %collective-permute-start.6 = (bf16[640,128]{1,0:T(8,128)(2,1)S(1)}, bf16[640,128]{1,0:T(8,128)(2,1)S(1)}, u32[]{:S(2)}, u32[]{:S(2)}) collective-permute-start(bf16[640,128]{1,0:T(8,128)(2,1)S(1)} %collective-permute-done.5.down_ref), channel_id=1, source_target_pairs={{0,1},{1,0},{2,3},{3,2},{4,5},{5,4},{6,7},{7,6},{8,9},{9,8},{10,11... | collective-permute-start | bytes 491528 | tf_op jit(solution)/shard_map/ppermute | solution.py:217
  19.3 0.6 %dynamic_slice.3 = s32[1,1]{0,1:T(1,128)} dynamic-slice(s32[32,8]{0,1:T(8,128)S(1)} %copy-done, s32[]{:T(128)S(6)} %select_n.28, s32[]{:T(128)S(6)} %select_n.29), dynamic_slice_sizes={1,1} | dynamic-slice | bytes 12 | tf_op jit(solution)/shard_map/dynamic_slice | solution.py:26
  20.5 0.0 collective-permute-done.4.mate_one_ref
  20.6 4.9 %collective-permute-done.3.up_ref = bf16[656,128]{1,0:T(8,128)(2,1)S(1)} collective-permute-done((bf16[656,128]{1,0:T(8,128)(2,1)S(1)}, bf16[656,128]{1,0:T(8,128)(2,1)S(1)}, u32[]{:S(2)}, u32[]{:S(2)}) %collective-permute-start.3) | collective-permute-done | bytes 167968 | tf_op jit(solution)/shard_map/ppermute | solution.py:213
  25.5 0.0 collective-permute-done.6.mate_down_ref
  25.5 1.6 %collective-permute-start.7 = (bf16[656,128]{1,0:T(8,128)(2,1)S(1)}, bf16[656,128]{1,0:T(8,128)(2,1)S(1)}, u32[]{:S(2)}, u32[]{:S(2)}) collective-permute-start(bf16[656,128]{1,0:T(8,128)(2,1)S(1)} %collective-permute-done.3.up_ref), channel_id=1, source_target_pairs={{0,1},{1,0},{2,3},{3,2},{4,5},{5,4},{6,7},{7,6},{8,9},{9,8},{10,11... | collective-permute-start | bytes 503816 | tf_op jit(solution)/shard_map/ppermute | solution.py:217
  27.7 0.4 %collective-permute-done.7.mate_up_ref = bf16[656,128]{1,0:T(8,128)(2,1)S(1)} collective-permute-done((bf16[656,128]{1,0:T(8,128)(2,1)S(1)}, bf16[656,128]{1,0:T(8,128)(2,1)S(1)}, u32[]{:S(2)}, u32[]{:S(2)}) %collective-permute-start.7) | collective-permute-done | bytes 167968 | tf_op jit(solution)/shard_map/ppermute | solution.py:217
  28.1 7.1 %columns.1 = (bf16[9,128,128]{2,1,0:T(8,128)(2,1)S(1)}, bf16[9,128,128]{2,1,0:T(8,128)(2,1)S(1)}) custom-call(s32[32,8]{1,0:T(8,128)} %copy.7.counts_ref, f32[1]{0:T(128)S(6)} %copy.9.mu_ref, bf16[20,128,128]{2,1,0:T(8,128)(2,1)S(1)} %get-tuple-element.16.local_ref, f32[16,128]{1,0:T(8,128)S(1)} %get-tuple-element.17.local_bits, ...), custom_call_target="tpu_custom_call" | custom-call | tf_op jit(solution)/shard_map/columns/pallas_call | solution.py:249
  35.2 0.5 %collective-permute-start.8 = (bf16[9,128,128]{2,1,0:T(8,128)(2,1)S(1)}, bf16[9,128,128]{2,1,0:T(8,128)(2,1)S(1)}, u32[]{:S(2)}, u32[]{:S(2)}) collective-permute-start(bf16[9,128,128]{2,1,0:T(8,128)(2,1)S(1)} %get-tuple-element.24.send_ref), channel_id=1, source_target_pairs={{0,1},{1,0},{2,3},{3,2},{4,5},{5,4},{6,7},{7,6},{8,9},{9,8},{10,11... | collective-permute-start | bytes 884744 | tf_op jit(solution)/shard_map/ppermute | solution.py:217
  35.6 1.8 %put.1 = bf16[3,9,128,128]{3,2,1,0:T(8,128)(2,1)} custom-call(s32[32,8]{1,0:T(8,128)} %copy.7.counts_ref, bf16[9,128,128]{2,1,0:T(8,128)(2,1)S(1)} %get-tuple-element.23.keep_ref, bf16[9,128,128]{2,1,0:T(8,128)(2,1)S(1)} %get-tuple-element.24.send_ref), custom_call_target="tpu_custom_call" | custom-call | tf_op jit(solution)/shard_map/put/pallas_call | solution.py:272
  37.4 0.0 collective-permute-done.8
  37.4 0.8 %bitcast_dynamic-update-slice_fusion = bf16[3,9,128,128]{3,2,1,0:T(8,128)(2,1)} fusion(bf16[3,9,128,128]{3,2,1,0:T(8,128)(2,1)} %put.1, s32[]{:T(128)S(6)} %select_n.34, bf16[9,128,128]{2,1,0:T(8,128)(2,1)S(1)} %collective-permute-done.8, pred[]{:T(512)} %bitcast), kind=kLoop, calls=%fused_computation | loop fusion | flops 147456 | bytes 590340 | tf_op jit(solution)/shard_map/dynamic_update_slice | solution.py:281
Async XLA Ops:
  0.0 4.2 %copy-start = (s32[32,8]{0,1:T(8,128)S(1)}, s32[32,8]{0,1:T(8,128)}, u32[]{:S(2)}) copy-start(s32[32,8]{0,1:T(8,128)} %param.6) | copy-start | bytes 3076
  0.0 4.9 %collective-permute-start.1 = (bf16[3,5,128,128]{3,2,1,0:T(8,128)(2,1)}, bf16[3,5,128,128]{3,2,1,0:T(8,128)(2,1)S(1)}, u32[]{:S(2)}, u32[]{:S(2)}) collective-permute-start(bf16[3,5,128,128]{3,2,1,0:T(8,128)(2,1)} %ham_ref.1), channel_id=1, source_target_pairs={{0,1},{1,0},{2,3},{3,2},{4,5},{5,4},{6,7},{7,6},{8,9},{9,8},{10,11... | collective-permute-start | bytes 1474568 | tf_op jit(solution)/shard_map/ppermute | solution.py:217
  3.2 1.7 %collective-permute-start = (s32[3,4]{1,0:T(4,128)}, s32[3,4]{1,0:T(4,128)S(1)}, u32[]{:S(2)}, u32[]{:S(2)}) collective-permute-start(s32[3,4]{1,0:T(4,128)} %bond_ref.1), channel_id=1, source_target_pairs={{0,1},{1,0},{2,3},{3,2},{4,5},{5,4},{6,7},{7,6},{8,9},{9,8},{10,11... | collective-permute-start | bytes 152 | tf_op jit(solution)/shard_map/ppermute | solution.py:217
  4.1 12.8 %collective-permute-start.2 = (bf16[1,5,128,128]{3,2,1,0:T(8,128)(2,1)S(1)}, bf16[1,5,128,128]{3,2,1,0:T(8,128)(2,1)S(1)}, u32[]{:S(2)}, u32[]{:S(2)}) collective-permute-start(bf16[1,5,128,128]{3,2,1,0:T(8,128)(2,1)S(1)} %slice.3), channel_id=1, source_target_pairs={{0,2},{1,3},{2,4},{3,5},{4,6},{5,7},{6,8},{7,9},{8,10},{9,11},{10,... | collective-permute-start | bytes 491528 | tf_op jit(solution)/shard_map/ppermute | solution.py:213
  6.2 11.8 %collective-permute-start.5 = (bf16[640,128]{1,0:T(8,128)(2,1)S(1)}, bf16[640,128]{1,0:T(8,128)(2,1)S(1)}, u32[]{:S(2)}, u32[]{:S(2)}) collective-permute-start(bf16[640,128]{1,0:T(8,128)(2,1)S(1)} %get-tuple-element.19), channel_id=1, source_target_pairs={{0,254},{1,255},{2,0},{3,1},{4,2},{5,3},{6,4},{7,5},{8,6},{9,7},{1... | collective-permute-start | bytes 491528 | tf_op jit(solution)/shard_map/ppermute | solution.py:213
  14.9 10.6 %collective-permute-start.3 = (bf16[656,128]{1,0:T(8,128)(2,1)S(1)}, bf16[656,128]{1,0:T(8,128)(2,1)S(1)}, u32[]{:S(2)}, u32[]{:S(2)}) collective-permute-start(bf16[656,128]{1,0:T(8,128)(2,1)S(1)} %get-tuple-element.18), channel_id=1, source_target_pairs={{0,2},{1,3},{2,4},{3,5},{4,6},{5,7},{6,8},{7,9},{8,10},{9,11},{10,... | collective-permute-start | bytes 503816 | tf_op jit(solution)/shard_map/ppermute | solution.py:213
  17.0 3.6 %collective-permute-start.4 = (bf16[1,5,128,128]{3,2,1,0:T(8,128)(2,1)S(1)}, bf16[1,5,128,128]{3,2,1,0:T(8,128)(2,1)S(1)}, u32[]{:S(2)}, u32[]{:S(2)}) collective-permute-start(bf16[1,5,128,128]{3,2,1,0:T(8,128)(2,1)S(1)} %collective-permute-done.2.one_ref), channel_id=1, source_target_pairs={{0,1},{1,0},{2,3},{3,2},{4,5},{5,4},{6,7},{7,6},{8,9},{9,8},{10,11... | collective-permute-start | bytes 491528 | tf_op jit(solution)/shard_map/ppermute | solution.py:217
  18.0 7.4 %collective-permute-start.6 = (bf16[640,128]{1,0:T(8,128)(2,1)S(1)}, bf16[640,128]{1,0:T(8,128)(2,1)S(1)}, u32[]{:S(2)}, u32[]{:S(2)}) collective-permute-start(bf16[640,128]{1,0:T(8,128)(2,1)S(1)} %collective-permute-done.5.down_ref), channel_id=1, source_target_pairs={{0,1},{1,0},{2,3},{3,2},{4,5},{5,4},{6,7},{7,6},{8,9},{9,8},{10,11... | collective-permute-start | bytes 491528 | tf_op jit(solution)/shard_map/ppermute | solution.py:217
  25.5 2.6 %collective-permute-start.7 = (bf16[656,128]{1,0:T(8,128)(2,1)S(1)}, bf16[656,128]{1,0:T(8,128)(2,1)S(1)}, u32[]{:S(2)}, u32[]{:S(2)}) collective-permute-start(bf16[656,128]{1,0:T(8,128)(2,1)S(1)} %collective-permute-done.3.up_ref), channel_id=1, source_target_pairs={{0,1},{1,0},{2,3},{3,2},{4,5},{5,4},{6,7},{7,6},{8,9},{9,8},{10,11... | collective-permute-start | bytes 503816 | tf_op jit(solution)/shard_map/ppermute | solution.py:217
  35.2 2.3 %collective-permute-start.8 = (bf16[9,128,128]{2,1,0:T(8,128)(2,1)S(1)}, bf16[9,128,128]{2,1,0:T(8,128)(2,1)S(1)}, u32[]{:S(2)}, u32[]{:S(2)}) collective-permute-start(bf16[9,128,128]{2,1,0:T(8,128)(2,1)S(1)} %get-tuple-element.24.send_ref), channel_id=1, source_target_pairs={{0,1},{1,0},{2,3},{3,2},{4,5},{5,4},{6,7},{7,6},{8,9},{9,8},{10,11... | collective-permute-start | bytes 884744 | tf_op jit(solution)/shard_map/ppermute | solution.py:217

commit v5 on v4

--- a/solution.py
+++ b/solution.py
@@ -30,8 +30,10 @@
     return jnp.where(low_count == 1, 2, 1) + parity
 
 
-def pack_kernel(counts_ref, bond_ref, mate_bond_ref, ham_ref, mate_ref, up_ref, down_ref, local_ref, bits_ref):
-    parity, low_count, _, _ = place(counts_ref)
+def pack_kernel(counts_ref, bond_ref, mate_bond_ref, ham_ref, mate_ref, up_ref, down_ref, local_ref, bits_ref, slot_ref, three_ref):
+    parity, low_count, count, _ = place(counts_ref)
+    three_ref[0] = jnp.where(count == 3, 1, 0)
+    slot_ref[0] = jnp.where(jnp.logical_and(count == 3, parity == 1), 0, 2)
     for t in range(CHIP_COLS):
         in_low = t < low_count
         slot = jnp.where(in_low, t, t - low_count)
@@ -225,26 +227,25 @@
     mate_bond = mate_of(bond_mask)
     mate_ham = mate_of(ham_columns)
     one_got = shift(ham_columns[0:1], 2)
-    up, down, local, bits = pl.pallas_call(
+    up, down, local, bits, slot, three = pl.pallas_call(
         pack_kernel,
         out_shape=(
             pltpu.VMEM((656, 128), BF16),
             pltpu.VMEM((640, 128), BF16),
             pltpu.VMEM((20, 128, 128), BF16),
             pltpu.VMEM((16, 128), F32),
+            jax.ShapeDtypeStruct((1,), jnp.int32),
+            jax.ShapeDtypeStruct((1,), jnp.int32),
         ),
         in_specs=[smem, vmem, vmem, vmem, vmem],
-        out_specs=(vmem,) * 4,
+        out_specs=(vmem,) * 4 + (smem,) * 2,
         name="pack",
     )(owned_counts, bond_mask, *on_chip(mate_bond), ham_columns, *on_chip(mate_ham))
     up_got = shift(up, 2)
     down_got = shift(down, -2)
     mate_one = mate_of(one_got)
     mate_down = mate_of(down_got)
-    parity, _, count, _ = place(owned_counts)
-    three = count == 3
-    slot = jnp.where(jnp.logical_and(three, parity == 1), 0, 2)
-    up_got, mate_one, mate_down, three, slot = lax.optimization_barrier((up_got, mate_one, mate_down, three, slot))
+    up_got, mate_one, mate_down = lax.optimization_barrier((up_got, mate_one, mate_down))
     mate_up = mate_of(up_got)
     keep, send = pl.pallas_call(
         main_kernel,
@@ -277,8 +278,8 @@
         scratch_shapes=[pltpu.VMEM((9, 128, 128), BF16), pltpu.SemaphoreType.DMA((3,))],
         name="put",
     )(owned_counts, *on_chip(keep, send))
-    last = jnp.where(three, got, jnp.zeros_like(got))
-    return lax.dynamic_update_slice(partial, last[None], (slot, 0, 0, 0))
+    last = jnp.where(three[0] == 1, got, jnp.zeros_like(got))
+    return lax.dynamic_update_slice(partial, last[None], (slot[0], 0, 0, 0))
 
 
 def solution(mesh):

time: 38.6 us -> 41.6 us (1.078)
  between operations: 1.38 us -> 3.22 us
  waiting for transfers between devices: 7.42 us -> 8.67 us
  local copies, waits for them, and re-layouts: 2.19 us -> 1.61 us
  Pallas kernels: 10.2 us -> 10.7 us
    ppermute x3, waiting for transfers between devices: 7.02 us -> 8.27 us  [shift(): lax.ppermute(value, AXES, [(s, (s + step) % size) for s in range(size)])]
    dynamic_slice x1 -> x0, local copies, waits for them, and re-layouts: 0.58 us -> none  [place(): return (parity, counts_ref[group, low], counts_ref[group, member], before)]
    pallas_call x1, Pallas kernels: 1.3 us -> 1.78 us  [body(): pl.pallas_call(pack_kernel, out_shape=(pltpu.VMEM((656, 128), BF16), pltp...]
  transfers between devices with their start and end apart: 9 -> 9, of which waited for: 4 -> 4; matrix products, arithmetic and copies ran while one was open for 6% -> 4% of each run, Pallas kernels for 8% -> 9%
where the time goes in v5:
time: 41.6 us; the launch traced here: 41.2 us
  starting transfers between devices  16.3 us (39%)
  Pallas kernels  10.7 us (26%)
  waiting for transfers between devices  8.67 us (21%)
  between operations  3.22 us (8%)
  local copies, waits for them, and re-layouts  1.61 us (4%)
  other arithmetic  0.78 us (2%)
    ppermute x3, starting transfers between devices, shift(): lax.ppermute(value, AXES, [(s, (s + step) % size) for s in range(size)])  8.76 us
    ppermute x3, waiting for transfers between devices, shift(): lax.ppermute(value, AXES, [(s, (s + step) % size) for s in range(size)])  8.27 us
    ppermute x6, starting transfers between devices, mate_of(): lax.ppermute(value, 'sub', [(s, s ^ 1) for s in range(lax.axis_size('sub'...  7.51 us
    pallas_call x1, Pallas kernels, body(): pl.pallas_call(main_kernel, out_shape=(pltpu.VMEM((9, 128, 128), BF16),)...  7.09 us
    pallas_call x1, Pallas kernels, body(): pl.pallas_call(pack_kernel, out_shape=(pltpu.VMEM((656, 128), BF16), pltp...  1.78 us
    pallas_call x1, Pallas kernels, body(): pl.pallas_call(put_kernel, out_shape=shape, in_specs=[smem, vmem, vmem],...  1.78 us
    slice x1, local copies, waits for them, and re-layouts, body(): one_got = shift(ham_columns[0:1], 2)  0.93 us
  transfers between devices with their start and end apart: 9, of which 4 were waited for; matrix products, arithmetic and copies ran while one was open for 4% of the time, Pallas kernels for 9%

profile of v5, /device:TPU:1, one launch (start us, length us, event | category | flops | bytes accessed | tf_op | source)
XLA Modules:
  0.0 41.2 jit_solution(2155379585648629448)
XLA Ops:
  0.0 0.0 copy-start
  0.0 3.2 %collective-permute-start.1 = (bf16[3,5,128,128]{3,2,1,0:T(8,128)(2,1)}, bf16[3,5,128,128]{3,2,1,0:T(8,128)(2,1)S(1)}, u32[]{:S(2)}, u32[]{:S(2)}) collective-permute-start(bf16[3,5,128,128]{3,2,1,0:T(8,128)(2,1)} %ham_ref.1), channel_id=1, source_target_pairs={{0,1},{1,0},{2,3},{3,2},{4,5},{5,4},{6,7},{7,6},{8,9},{9,8},{10,11... | collective-permute-start | bytes 1474568 | tf_op jit(solution)/shard_map/ppermute | solution.py:219
  3.2 0.0 collective-permute-start
  3.2 0.9 %slice.3 = bf16[1,5,128,128]{3,2,1,0:T(8,128)(2,1)S(1)} slice(bf16[3,5,128,128]{3,2,1,0:T(8,128)(2,1)} %ham_ref.1), slice={[0:1], [0:5], [0:128], [0:128]} | slice | bytes 327680 | tf_op jit(solution)/shard_map/slice | solution.py:229
  4.1 0.1 collective-permute-start.2
  4.2 0.0 copy-done
  4.2 0.7 %copy.7.counts_ref = s32[32,8]{1,0:T(8,128)} copy(s32[32,8]{0,1:T(8,128)S(1)} %copy-done) | data formatting | bytes 2048 | tf_op args[2]
  4.9 0.0 collective-permute-done.mate_bond_ref
  4.9 0.0 collective-permute-done.1.mate_ref
  4.9 1.8 %pack.1 = (bf16[656,128]{1,0:T(8,128)(2,1)S(1)}, bf16[640,128]{1,0:T(8,128)(2,1)S(1)}, bf16[20,128,128]{2,1,0:T(8,128)(2,1)S(1)}, f32[16,128]{1,0:T(8,128)S(1)}, s32[1]{0:T(128)}, /*index=5*/s32[1]{0:T(128)}) custom-call(s32[32,8]{1,0:T(8,128)} %copy.7.counts_ref, s32[3,4]{1,0:T(4,128)} %bond_ref.1, s32[3,4]{1,0:T(4,128)S(1)} %collective-permute-done.mate_bond_ref, ...), custom_call_target="tpu_custom_call" | custom-call | tf_op jit(solution)/shard_map/pack/pallas_call | solution.py:230
  6.7 8.7 %collective-permute-start.5 = (bf16[640,128]{1,0:T(8,128)(2,1)S(1)}, bf16[640,128]{1,0:T(8,128)(2,1)S(1)}, u32[]{:S(2)}, u32[]{:S(2)}) collective-permute-start(bf16[640,128]{1,0:T(8,128)(2,1)S(1)} %get-tuple-element.19), channel_id=1, source_target_pairs={{0,254},{1,255},{2,0},{3,1},{4,2},{5,3},{6,4},{7,5},{8,6},{9,7},{1... | collective-permute-start | bytes 491528 | tf_op jit(solution)/shard_map/ppermute | solution.py:215
  15.4 0.0 collective-permute-start.3
  15.4 1.6 %collective-permute-done.2.one_ref = bf16[1,5,128,128]{3,2,1,0:T(8,128)(2,1)S(1)} collective-permute-done((bf16[1,5,128,128]{3,2,1,0:T(8,128)(2,1)S(1)}, bf16[1,5,128,128]{3,2,1,0:T(8,128)(2,1)S(1)}, u32[]{:S(2)}, u32[]{:S(2)}) %collective-permute-start.2) | collective-permute-done | bytes 163872 | tf_op jit(solution)/shard_map/ppermute | solution.py:215
  17.0 1.0 %collective-permute-start.4 = (bf16[1,5,128,128]{3,2,1,0:T(8,128)(2,1)S(1)}, bf16[1,5,128,128]{3,2,1,0:T(8,128)(2,1)S(1)}, u32[]{:S(2)}, u32[]{:S(2)}) collective-permute-start(bf16[1,5,128,128]{3,2,1,0:T(8,128)(2,1)S(1)} %collective-permute-done.2.one_ref), channel_id=1, source_target_pairs={{0,1},{1,0},{2,3},{3,2},{4,5},{5,4},{6,7},{7,6},{8,9},{9,8},{10,11... | collective-permute-start | bytes 491528 | tf_op jit(solution)/shard_map/ppermute | solution.py:219
  18.0 0.6 %collective-permute-done.5.down_ref = bf16[640,128]{1,0:T(8,128)(2,1)S(1)} collective-permute-done((bf16[640,128]{1,0:T(8,128)(2,1)S(1)}, bf16[640,128]{1,0:T(8,128)(2,1)S(1)}, u32[]{:S(2)}, u32[]{:S(2)}) %collective-permute-start.5) | collective-permute-done | bytes 163872 | tf_op jit(solution)/shard_map/ppermute | solution.py:215
  18.5 1.3 %collective-permute-start.6 = (bf16[640,128]{1,0:T(8,128)(2,1)S(1)}, bf16[640,128]{1,0:T(8,128)(2,1)S(1)}, u32[]{:S(2)}, u32[]{:S(2)}) collective-permute-start(bf16[640,128]{1,0:T(8,128)(2,1)S(1)} %collective-permute-done.5.down_ref), channel_id=1, source_target_pairs={{0,1},{1,0},{2,3},{3,2},{4,5},{5,4},{6,7},{7,6},{8,9},{9,8},{10,11... | collective-permute-start | bytes 491528 | tf_op jit(solution)/shard_map/ppermute | solution.py:219
  19.8 0.0 collective-permute-done.4.mate_one_ref
  19.8 6.2 %collective-permute-done.3.up_ref = bf16[656,128]{1,0:T(8,128)(2,1)S(1)} collective-permute-done((bf16[656,128]{1,0:T(8,128)(2,1)S(1)}, bf16[656,128]{1,0:T(8,128)(2,1)S(1)}, u32[]{:S(2)}, u32[]{:S(2)}) %collective-permute-start.3) | collective-permute-done | bytes 167968 | tf_op jit(solution)/shard_map/ppermute | solution.py:215
  26.0 0.0 collective-permute-done.6.mate_down_ref
  26.0 1.6 %collective-permute-start.7 = (bf16[656,128]{1,0:T(8,128)(2,1)S(1)}, bf16[656,128]{1,0:T(8,128)(2,1)S(1)}, u32[]{:S(2)}, u32[]{:S(2)}) collective-permute-start(bf16[656,128]{1,0:T(8,128)(2,1)S(1)} %collective-permute-done.3.up_ref), channel_id=1, source_target_pairs={{0,1},{1,0},{2,3},{3,2},{4,5},{5,4},{6,7},{7,6},{8,9},{9,8},{10,11... | collective-permute-start | bytes 503816 | tf_op jit(solution)/shard_map/ppermute | solution.py:219
  28.2 0.4 collective-permute-done.7.mate_up_ref
  28.6 7.1 %columns.1 = (bf16[9,128,128]{2,1,0:T(8,128)(2,1)S(1)}, bf16[9,128,128]{2,1,0:T(8,128)(2,1)S(1)}) custom-call(s32[32,8]{1,0:T(8,128)} %copy.7.counts_ref, f32[1]{0:T(128)S(6)} %copy.9.mu_ref, bf16[20,128,128]{2,1,0:T(8,128)(2,1)S(1)} %get-tuple-element.16.local_ref, f32[16,128]{1,0:T(8,128)S(1)} %get-tuple-element.17.local_bits, ...), custom_call_target="tpu_custom_call" | custom-call | tf_op jit(solution)/shard_map/columns/pallas_call | solution.py:250
  35.6 0.5 %collective-permute-start.8 = (bf16[9,128,128]{2,1,0:T(8,128)(2,1)S(1)}, bf16[9,128,128]{2,1,0:T(8,128)(2,1)S(1)}, u32[]{:S(2)}, u32[]{:S(2)}) collective-permute-start(bf16[9,128,128]{2,1,0:T(8,128)(2,1)S(1)} %get-tuple-element.24.send_ref), channel_id=1, source_target_pairs={{0,1},{1,0},{2,3},{3,2},{4,5},{5,4},{6,7},{7,6},{8,9},{9,8},{10,11... | collective-permute-start | bytes 884744 | tf_op jit(solution)/shard_map/ppermute | solution.py:219
  38.6 1.8 %put.1 = bf16[3,9,128,128]{3,2,1,0:T(8,128)(2,1)} custom-call(s32[32,8]{1,0:T(8,128)} %copy.7.counts_ref, bf16[9,128,128]{2,1,0:T(8,128)(2,1)S(1)} %get-tuple-element.23.keep_ref, bf16[9,128,128]{2,1,0:T(8,128)(2,1)S(1)} %get-tuple-element.24.send_ref), custom_call_target="tpu_custom_call" | custom-call | tf_op jit(solution)/shard_map/put/pallas_call | solution.py:273
  40.4 0.0 collective-permute-done.8
  40.4 0.8 %bitcast_dynamic-update-slice_fusion = bf16[3,9,128,128]{3,2,1,0:T(8,128)(2,1)} fusion(bf16[3,9,128,128]{3,2,1,0:T(8,128)(2,1)} %put.1, s32[]{:T(128)S(6)} %select_n.13, bf16[9,128,128]{2,1,0:T(8,128)(2,1)S(1)} %collective-permute-done.8, pred[]{:T(512)} %bitcast), kind=kLoop, calls=%fused_computation | loop fusion | flops 147456 | bytes 590340 | tf_op jit(solution)/shard_map/dynamic_update_slice | solution.py:282
Async XLA Ops:
  0.0 4.2 %copy-start = (s32[32,8]{0,1:T(8,128)S(1)}, s32[32,8]{0,1:T(8,128)}, u32[]{:S(2)}) copy-start(s32[32,8]{0,1:T(8,128)} %param.6) | copy-start | bytes 3076
  0.0 4.9 %collective-permute-start.1 = (bf16[3,5,128,128]{3,2,1,0:T(8,128)(2,1)}, bf16[3,5,128,128]{3,2,1,0:T(8,128)(2,1)S(1)}, u32[]{:S(2)}, u32[]{:S(2)}) collective-permute-start(bf16[3,5,128,128]{3,2,1,0:T(8,128)(2,1)} %ham_ref.1), channel_id=1, source_target_pairs={{0,1},{1,0},{2,3},{3,2},{4,5},{5,4},{6,7},{7,6},{8,9},{9,8},{10,11... | collective-permute-start | bytes 1474568 | tf_op jit(solution)/shard_map/ppermute | solution.py:219
  3.2 1.7 %collective-permute-start = (s32[3,4]{1,0:T(4,128)}, s32[3,4]{1,0:T(4,128)S(1)}, u32[]{:S(2)}, u32[]{:S(2)}) collective-permute-start(s32[3,4]{1,0:T(4,128)} %bond_ref.1), channel_id=1, source_target_pairs={{0,1},{1,0},{2,3},{3,2},{4,5},{5,4},{6,7},{7,6},{8,9},{9,8},{10,11... | collective-permute-start | bytes 152 | tf_op jit(solution)/shard_map/ppermute | solution.py:219
  4.1 12.8 %collective-permute-start.2 = (bf16[1,5,128,128]{3,2,1,0:T(8,128)(2,1)S(1)}, bf16[1,5,128,128]{3,2,1,0:T(8,128)(2,1)S(1)}, u32[]{:S(2)}, u32[]{:S(2)}) collective-permute-start(bf16[1,5,128,128]{3,2,1,0:T(8,128)(2,1)S(1)} %slice.3), channel_id=1, source_target_pairs={{0,2},{1,3},{2,4},{3,5},{4,6},{5,7},{6,8},{7,9},{8,10},{9,11},{10,... | collective-permute-start | bytes 491528 | tf_op jit(solution)/shard_map/ppermute | solution.py:215
  6.7 11.8 %collective-permute-start.5 = (bf16[640,128]{1,0:T(8,128)(2,1)S(1)}, bf16[640,128]{1,0:T(8,128)(2,1)S(1)}, u32[]{:S(2)}, u32[]{:S(2)}) collective-permute-start(bf16[640,128]{1,0:T(8,128)(2,1)S(1)} %get-tuple-element.19), channel_id=1, source_target_pairs={{0,254},{1,255},{2,0},{3,1},{4,2},{5,3},{6,4},{7,5},{8,6},{9,7},{1... | collective-permute-start | bytes 491528 | tf_op jit(solution)/shard_map/ppermute | solution.py:215
  15.4 10.6 %collective-permute-start.3 = (bf16[656,128]{1,0:T(8,128)(2,1)S(1)}, bf16[656,128]{1,0:T(8,128)(2,1)S(1)}, u32[]{:S(2)}, u32[]{:S(2)}) collective-permute-start(bf16[656,128]{1,0:T(8,128)(2,1)S(1)} %get-tuple-element.18), channel_id=1, source_target_pairs={{0,2},{1,3},{2,4},{3,5},{4,6},{5,7},{6,8},{7,9},{8,10},{9,11},{10,... | collective-permute-start | bytes 503816 | tf_op jit(solution)/shard_map/ppermute | solution.py:215
  17.0 2.8 %collective-permute-start.4 = (bf16[1,5,128,128]{3,2,1,0:T(8,128)(2,1)S(1)}, bf16[1,5,128,128]{3,2,1,0:T(8,128)(2,1)S(1)}, u32[]{:S(2)}, u32[]{:S(2)}) collective-permute-start(bf16[1,5,128,128]{3,2,1,0:T(8,128)(2,1)S(1)} %collective-permute-done.2.one_ref), channel_id=1, source_target_pairs={{0,1},{1,0},{2,3},{3,2},{4,5},{5,4},{6,7},{7,6},{8,9},{9,8},{10,11... | collective-permute-start | bytes 491528 | tf_op jit(solution)/shard_map/ppermute | solution.py:219
  18.5 7.4 %collective-permute-start.6 = (bf16[640,128]{1,0:T(8,128)(2,1)S(1)}, bf16[640,128]{1,0:T(8,128)(2,1)S(1)}, u32[]{:S(2)}, u32[]{:S(2)}) collective-permute-start(bf16[640,128]{1,0:T(8,128)(2,1)S(1)} %collective-permute-done.5.down_ref), channel_id=1, source_target_pairs={{0,1},{1,0},{2,3},{3,2},{4,5},{5,4},{6,7},{7,6},{8,9},{9,8},{10,11... | collective-permute-start | bytes 491528 | tf_op jit(solution)/shard_map/ppermute | solution.py:219
  26.0 2.6 %collective-permute-start.7 = (bf16[656,128]{1,0:T(8,128)(2,1)S(1)}, bf16[656,128]{1,0:T(8,128)(2,1)S(1)}, u32[]{:S(2)}, u32[]{:S(2)}) collective-permute-start(bf16[656,128]{1,0:T(8,128)(2,1)S(1)} %collective-permute-done.3.up_ref), channel_id=1, source_target_pairs={{0,1},{1,0},{2,3},{3,2},{4,5},{5,4},{6,7},{7,6},{8,9},{9,8},{10,11... | collective-permute-start | bytes 503816 | tf_op jit(solution)/shard_map/ppermute | solution.py:219
  35.6 4.8 %collective-permute-start.8 = (bf16[9,128,128]{2,1,0:T(8,128)(2,1)S(1)}, bf16[9,128,128]{2,1,0:T(8,128)(2,1)S(1)}, u32[]{:S(2)}, u32[]{:S(2)}) collective-permute-start(bf16[9,128,128]{2,1,0:T(8,128)(2,1)S(1)} %get-tuple-element.24.send_ref), channel_id=1, source_target_pairs={{0,1},{1,0},{2,3},{3,2},{4,5},{5,4},{6,7},{7,6},{8,9},{9,8},{10,11... | collective-permute-start | bytes 884744 | tf_op jit(solution)/shard_map/ppermute | solution.py:219
